TPU v7x, 128 devices: a whole 4x4x4 slice. The times are simulated.
128 devices in a mesh: band: 32 (over z, y, x_hi), grid: 4 (over x_lo, core).
Axes of the slice: x: 4 (x_hi: 2, x_lo: 2; x = x_hi * 2 + x_lo), y: 4, z: 4, core: 2. Of those that a mesh axis runs over, the one named last changes fastest.
Arguments:
- orbitals: float32 [128, 110592], P('band', 'grid'), may hold values from -6 to 6
Outputs:
- exchange_vectors: float32 [128, 110592], P('band', 'grid')
- margin: float32 [128, 128], P('grid', 'band')
All inputs are finite; a program needn't handle non-finite values.
Results may differ from a plain program's by a relative error of at most 0.00012.
Values sent between devices are 32-bit elements; how exact they have to be, the bound alone decides.
A program may use at most 128 MiB of HBM per device.

v0:
```python
import functools

import jax
import jax.numpy as jnp
import numpy as np
from jax import lax
from jax.experimental import pallas as pl
from jax.experimental.pallas import tpu as pltpu
from jax.sharding import PartitionSpec as P


def kernel_values(ng):
    freqs = ((np.arange(ng) + ng // 2) % ng - ng // 2).astype(np.float32)
    sq = freqs[: ng // 2 + 1, None, None] ** 2 + freqs[None, :, None] ** 2 + freqs[None, None, :] ** 2
    safe = np.where(sq > 0, sq, np.float32(1.0))
    return np.where(sq > 0, 40.0 * (1.0 - np.exp(-sq / 16.0)) / safe, 0.0)


def hartley(ng):
    k = np.arange(ng)
    ang = (k[:, None] * k[None, :] % ng) * (2.0 * np.pi / ng)
    return np.cos(ang) + np.sin(ang)


def split_const(table):
    table = np.asarray(table, np.float32)
    hi = table.astype(jnp.bfloat16)
    lo = (table - hi.astype(np.float32)).astype(jnp.bfloat16)
    return hi, lo


def rfft(xs):
    n = len(xs)
    if n == 3:
        s = xs[1] + xs[2]
        d = xs[1] - xs[2]
        return [(xs[0] + s, None), (xs[0] - 0.5 * s, d * (-np.sqrt(3.0) / 2))]
    even, odd = rfft(xs[0::2]), rfft(xs[1::2])
    half = n // 2
    out = [None] * (half + 1)
    for k in range(half // 2 + 1):
        er, ei = even[k]
        orr, oi = odd[k]
        if k == 0:
            out[0] = (er + orr, None)
            out[half] = (er - orr, None)
            continue
        c, s = np.cos(2 * np.pi * k / n), -np.sin(2 * np.pi * k / n)
        if 2 * k == half:
            out[k] = (er, -orr)
            continue
        tr, ti = cmul(orr, oi, c, s)
        out[k] = (er + tr, addo(ei, ti))
        out[half - k] = (er - tr, subo(ti, ei))
    return out


def addo(a, b):
    return b if a is None else a + b


def subo(a, b):
    return a if b is None else a - b


def cmul(r, i, c, s):
    if i is None:
        return r * c, r * s
    if abs(abs(c) - abs(s)) < 1e-9:
        if s < 0 < c:
            return (r + i) * c, (i - r) * c
        return (r - i) * c, (r + i) * c
    return r * c - i * s, r * s + i * c


def irfft(spec, n):
    if n == 3:
        dc, (r, i) = spec[0][0], spec[1]
        base = dc - r
        t = i * np.sqrt(3.0)
        return [dc + 2.0 * r, base - t, base + t]
    half = n // 2
    even, odd = [None] * (half // 2 + 1), [None] * (half // 2 + 1)
    for k in range(half // 2 + 1):
        yr, yi = spec[k]
        if k == 0:
            hr = spec[half][0]
            even[0] = (yr + hr, None)
            odd[0] = (yr - hr, None)
            continue
        if 2 * k == half:
            even[k] = (yr + yr, None)
            odd[k] = (-(yi + yi), None)
            continue
        zr, zi = spec[half - k]
        er, ei = yr + zr, yi - zi
        dr, di = yr - zr, yi + zi
        c, s = np.cos(2 * np.pi * k / n), np.sin(2 * np.pi * k / n)
        even[k] = (er, ei)
        odd[k] = cmul(dr, di, c, s)
    ev, od = irfft(even, half), irfft(odd, half)
    out = [None] * n
    out[0::2], out[1::2] = ev, od
    return out


def split(v):
    hi = v.astype(jnp.bfloat16)
    lo = (v - hi.astype(jnp.float32)).astype(jnp.bfloat16)
    return hi, lo


def mm(a, b):
    return jnp.dot(a, b, preferred_element_type=jnp.float32)


def solve_kernel(ng, own_ref, k1_ref, k2_ref, zh_ref, zl_ref, ty_ref, sel_ref, s_ref, o_ref,
                 buf, amp, acc, work, vec, recv, rsem, ssem, nsem, osem, orsem, lsem):
    planes, _, width = own_ref.shape
    me = lax.axis_index("grid")
    band, nband = lax.axis_index("band"), lax.axis_size("band")
    chip, core = me // 2, me % 2
    sib = chip * 2 + (1 - core)
    cross = (1 - chip) * 2 + core
    far = (1 - chip) * 2 + (1 - core)
    above, below = (band + 1) % nband, (band + nband - 1) % nband
    mesh_id = pl.DeviceIdType.MESH

    def remote(src, dst, send, recv_sem, device):
        return pltpu.make_async_remote_copy(
            src_ref=src, dst_ref=dst, send_sem=send, recv_sem=recv_sem,
            device_id=device, device_id_type=mesh_id,
        )

    def share(blk, lane, slot, src, target):
        return remote(src, buf.at[blk, slot], ssem.at[blk, lane], rsem.at[blk, slot], (band, target))

    barrier = pltpu.get_barrier_semaphore()
    for device in ((band, sib), (band, cross), (band, far), (above, me), (below, me)):
        pl.semaphore_signal(barrier, inc=1, device_id=device, device_id_type=mesh_id)
    pl.semaphore_wait(barrier, 5)

    share(0, 1, me, own_ref, cross).start()
    share(0, 0, me, own_ref, sib).start()
    remote(own_ref, buf.at[1, me], nsem.at[0], rsem.at[1, me], (above, me)).start()
    remote(own_ref, buf.at[2, me], nsem.at[1], rsem.at[2, me], (below, me)).start()
    local = pltpu.make_async_copy(own_ref, buf.at[0, me], lsem)
    local.start()

    def arrived(blk, slot):
        share(blk, 0, slot, own_ref, sib).wait_recv()

    def relay(blk):
        arrived(blk, cross)
        share(blk, 2, cross, buf.at[blk, cross], sib).start()

    def spread(blk):
        arrived(blk, me)
        share(blk, 1, me, buf.at[blk, me], cross).start()
        share(blk, 0, me, buf.at[blk, me], sib).start()

    def ztrans(v):
        hi, lo = split(v)
        return mm(hi, zh_ref[...]) + mm(lo, zh_ref[...]) + mm(hi, zl_ref[...])

    def ytrans(v):
        hi, lo = split(v)
        return mm(ty_ref[...], jnp.concatenate([hi, lo, hi], axis=0))

    def slot_of(s):
        return ((chip + s // 2) % 2) * 2 + (core + s % 2) % 2

    def amplitude(slot):
        hi, lo = split(buf[0, slot].reshape(planes * ng, width))
        amp[slot] = (mm(hi, sel_ref[me]) + mm(lo, sel_ref[me])).reshape(planes, ng, width)

    def forward(blk, s):
        slot = slot_of(s)

        @pl.when(s == 1)
        def _():
            arrived(blk, sib)

        @pl.when(jnp.logical_and(blk == 0, s == 2))
        def _():
            relay(0)
            spread(1)

        @pl.when(s == 3)
        def _():
            arrived(blk, far)

        @pl.when(blk == 0)
        def _():
            amplitude(slot)

        p = (amp[slot] * buf[blk, slot]).reshape(planes * ng, width)
        q = ztrans(p).reshape(planes, ng, width)
        for r in range(planes):
            work[slot, r] = ytrans(q[r])

    def conv(vals, kern):
        spec = rfft(vals)
        out = []
        for k, (re, im) in enumerate(spec):
            kv = kern(k)
            out.append((re * kv, None if im is None else im * kv))
        return irfft(out, ng)

    def xconv(t):
        order = [(g, h, r) for g in range(4) for h in range(2) for r in range(planes)]
        for i in range(2):
            rows = pl.ds(pl.multiple_of(t * 16 + 8 * i, 8), 8)
            res = conv([work[g, r, rows, h * 128:h * 128 + 128] for g, h, r in order],
                       lambda k: k1_ref[k, rows, :])
            for (g, h, r), v in zip(order, res):
                work[g, r, rows, h * 128:h * 128 + 128] = v
        ra = pl.ds(pl.multiple_of(t * 16, 8), 8)
        rb = pl.ds(pl.multiple_of(t * 16 + 8, 8), 8)
        left = lax.broadcasted_iota(jnp.int32, (8, 128), 1) < 64

        def half(g, h, r):
            u, w = work[g, r, ra, 256:384], work[g, r, rb, 256:384]
            if h == 0:
                return jnp.where(left, u, pltpu.roll(w, 64, 1))
            return jnp.where(left, pltpu.roll(u, 64, 1), w)

        rk = pl.ds(pl.multiple_of(t * 8, 8), 8)
        res = dict(zip(order, conv([half(*o) for o in order], lambda k: k2_ref[k, rk, :])))
        for g in range(4):
            for r in range(planes):
                a, b = res[(g, 0, r)], res[(g, 1, r)]
                work[g, r, ra, 256:384] = jnp.where(left, a, pltpu.roll(b, 64, 1))
                work[g, r, rb, 256:384] = jnp.where(left, pltpu.roll(a, 64, 1), b)

    def push(slot):
        return remote(vec.at[slot], recv.at[me], osem.at[slot], orsem.at[me], (band, slot))

    def inverse(blk, s):
        slot = ((chip + 1 - s // 2) % 2) * 2 + (core + s % 2 + s // 2) % 2
        q = jnp.concatenate([ytrans(work[slot, r]) for r in range(planes)], axis=0)
        w = ztrans(q).reshape(planes, ng, width) * buf[blk, slot]

        @pl.when(blk == 0)
        def _():
            acc[slot] = w

        @pl.when(blk == 1)
        def _():
            acc[slot] += w

        @pl.when(blk == 2)
        def _():
            hi, lo = split((acc[slot] + w).reshape(planes * ng, width))
            out = -(mm(hi, s_ref[...]) + mm(lo, s_ref[...]))
            vec[slot] = out.reshape(planes, ng, s_ref.shape[-1])

            @pl.when(s < 3)
            def _():
                push(slot).start()

    def block(blk, _):
        @pl.when(blk == 0)
        def _():
            local.wait()

        @pl.when(blk > 0)
        def _():
            relay(blk)

        @pl.when(blk == 1)
        def _():
            spread(2)

        def fwd(s, _):
            forward(blk, s)
            return 0

        def mid(t, _):
            xconv(t)
            return 0

        def inv(s, _):
            inverse(blk, s)
            return 0

        lax.fori_loop(0, 4, fwd, 0)
        lax.fori_loop(0, ng // 16, mid, 0)
        lax.fori_loop(0, 4, inv, 0)
        return 0

    lax.fori_loop(0, 3, block, 0)

    o_ref[me] = vec[me]
    for slot in (sib, cross, far):
        remote(vec.at[slot], recv.at[slot], osem.at[slot], orsem.at[slot], (band, slot)).wait()
        o_ref[slot] = recv[slot]
    for blk in range(3):
        for lane, target in ((0, sib), (1, cross), (2, sib)):
            share(blk, lane, me, own_ref, target).wait_send()
    remote(own_ref, buf.at[1, me], nsem.at[0], rsem.at[1, me], (above, me)).wait_send()
    remote(own_ref, buf.at[2, me], nsem.at[1], rsem.at[2, me], (below, me)).wait_send()


def lane_tables(ng, bands):
    w = bands * ng
    half, bz = [], []
    for lo, hi in ((0, 128), (128, w)):
        for h in range(2):
            half.append(np.full(hi - lo, h))
            bz.append(np.arange(lo, hi))
    half, bz = np.concatenate(half), np.concatenate(bz)
    return half, bz // ng, bz % ng


def solve(own, bands, groups):
    planes, ng, width = own.shape
    half, bnd, zed = lane_tables(ng, bands)
    ht = hartley(ng)
    th, tl = split_const(ht)
    same = (half[:, None] == half[None, :])
    zh, zl = split_const(np.where(same & (bnd[:, None] == bnd[None, :]), ht[zed[:, None], zed[None, :]], 0.0))
    ty = np.concatenate([th, th, tl], axis=1)
    copyz = same & (zed[:, None] == zed[None, :])
    sel = np.stack([copyz & (bnd[:, None] == g) for g in range(groups)]).astype(np.float32)
    s = np.zeros((width, 128), np.float32)
    s[np.arange(width), half * ng + zed] = 1.0
    kv = kernel_values(ng).astype(np.float32) / np.float32(ng**3)
    kb = np.tile(kv, (1, 1, bands))
    k1 = kb[:, :, :128]
    rest = kb[:, :, 128:].reshape(kb.shape[0], ng // 16, 2, 8, 64)
    k2 = np.concatenate([rest[:, :, 0], rest[:, :, 1]], axis=-1).reshape(kb.shape[0], ng // 2, 128)
    consts = [k1, k2, zh, zl, ty, sel.astype(jnp.bfloat16), s.astype(jnp.bfloat16)]
    full = (groups, planes, ng, width)
    f32, dma = jnp.float32, pltpu.SemaphoreType.DMA
    return pl.pallas_call(
        functools.partial(solve_kernel, ng),
        out_shape=jax.ShapeDtypeStruct((groups, planes, ng, 128), f32),
        in_specs=[pl.BlockSpec(memory_space=pltpu.VMEM)] * 8,
        out_specs=pl.BlockSpec(memory_space=pltpu.VMEM),
        scratch_shapes=[
            pltpu.VMEM((3,) + full, f32), pltpu.VMEM(full, f32), pltpu.VMEM(full, f32), pltpu.VMEM(full, f32),
            pltpu.VMEM((groups, planes, ng, 128), f32), pltpu.VMEM((groups, planes, ng, 128), f32),
            dma((3, groups)), dma((3, 3)), dma((2,)), dma((groups,)), dma((groups,)), dma(()),
        ],
        compiler_params=pltpu.CompilerParams(
            vmem_limit_bytes=56 * 1024 * 1024, collective_id=0, has_side_effects=True
        ),
        cost_estimate=pl.CostEstimate(flops=10**11, bytes_accessed=10**7, transcendentals=0),
        name="solve",
    )(own, *[jnp.asarray(c) for c in consts])


def on_device(orbitals):
    groups = lax.axis_size("grid")
    bands, local = orbitals.shape
    ncell = local * groups
    ng = round(ncell ** (1 / 3))
    xs = local // (ng * ng)
    planes = xs // 2
    t = orbitals.reshape(bands, 2, planes, ng, ng).transpose(2, 3, 1, 0, 4).reshape(planes, ng, 2, bands * ng)
    own = jnp.concatenate([t[:, :, 0, :128], t[:, :, 1, :128], t[:, :, 0, 128:], t[:, :, 1, 128:]], axis=-1)
    out = solve(own, bands, groups)
    vec = out[..., : 2 * ng].reshape(groups, planes, ng, 2, ng).transpose(0, 3, 1, 2, 4)
    vectors = vec.reshape(bands, local)
    terms = (
        lax.dot_general(
            lax.all_gather(orbitals, "band", axis=0, tiled=True),
            vectors,
            (((1,), (1,)), ((), ())),
            precision=lax.Precision.HIGHEST,
            preferred_element_type=jnp.float32,
        )
        / ncell
    )
    margin = lax.psum_scatter(terms, "grid", scatter_dimension=0, tiled=True)
    return (vectors, margin)


def solution(mesh):
    return jax.shard_map(
        on_device,
        mesh=mesh,
        in_specs=(P("band", "grid"),),
        out_specs=(P("band", "grid"), P("grid", "band")),
        check_vma=False,
    )
```

profile of v0, /device:TPU:1, one launch (start us, length us, event | category | flops | bytes accessed | tf_op | source)
XLA Modules:
  0.0 226.2 jit_solution(4035825076739382187)
XLA Ops:
  7.2 0.0 all-gather.3.cloned.1.call-start
  7.2 0.7 all-gather.3.cloned.1.call-update
  7.9 0.0 reduce-scatter.4.cloned.1.call-start
  7.9 1.6 reshape.16
  9.5 0.8 copy.17
  10.3 0.5 reshape.17
  10.9 0.9 pad_maximum_fusion.own_ref
  11.7 91.1 %solve.1 = f32[4,6,48,128]{3,2,1,0:T(8,128)} custom-call(f32[6,48,384]{2,1,0:T(8,128)} %pad_maximum_fusion.own_ref, f32[25,48,128]{2,1,0:T(8,128)} %constant.17.clone.k1_ref, f32[25,24,128]{2,1,0:T(8,128)} %constant.18.clone.k2_ref, bf16[384,384]{1,0:T(8,128)(2,1)} %constant.19.clone.zh_ref, bf16[384,384]{1,0:T(8,128)(2,1)} %constant.20.clone.zl_ref, ...), custom_call_target="tpu_custom_call" | custom-call | flops 99999997952 | bytes 10000000 | tf_op jit(solution)/shard_map/solve/pallas_call | solution.py:336
  102.8 1.7 reshape.18
  104.6 0.1 copy.13
  104.7 0.8 reshape.19
  105.5 0.0 copy-start
  105.5 67.8 %all-gather.3.cloned.1.call-done = f32[32,4,27648]{2,1,0:T(4,128)} async-done(((f32[1,4,27648]{2,1,0:T(4,128)}), f32[32,4,27648]{2,1,0:T(4,128)}) %all-gather.3.cloned.1.call-update) | async-done | bytes 14155792 | tf_op jit(solution)/shard_map/all_gather | solution.py:368
  173.3 14.1 %reshape.21 = f32[128,27648]{1,0:T(8,128)} reshape(f32[32,4,27648]{2,1,0:T(4,128)} %all-gather.3.cloned.1.call-done) | data formatting | bytes 28311552
  187.4 0.0 copy-done
  187.4 13.6 %fusion = f32[128,4]{0,1:T(4,128)S(1)} fusion(f32[4,27648]{1,0:T(4,128)S(1)} %reshape.19, f32[128,27648]{1,0:T(8,128)} %reshape.21), kind=kOutput, calls=%fused_computation.2 | convolution fusion | flops 169869824 | bytes 14600192 | tf_op jit(solution)/shard_map/dot_general | solution.py:367
  201.0 0.8 copy.14
  201.7 0.0 reduce-scatter.4.cloned.1.call-update
  201.8 16.2 %reduce-scatter.4.cloned.1.call-done = f32[32,4]{1,0:T(8,128)} async-done(((f32[128,4]{1,0:T(8,128)}), f32[32,4]{1,0:T(8,128)}) %reduce-scatter.4.cloned.1.call-update) | async-done | bytes 528
  218.0 1.4 copy.15
  (2 shorter events, 0.0 us)
Async XLA Ops:
  7.2 166.1 %all-gather.3.cloned.1.call-start = ((), (), s32[]{:S(2)}) async-start(), calls=%async_computation.1 | async-start | bytes 14598144 | tf_op jit(solution)/shard_map/all_gather | solution.py:368
  7.9 210.1 %reduce-scatter.4.cloned.1.call-start = ((), (), s32[]{:S(2)}) async-start(), calls=%async_computation.2 | async-start | bytes 81920
  105.5 81.9 %copy-start = (f32[4,27648]{1,0:T(4,128)}, f32[4,27648]{1,0:T(4,128)S(1)}, u32[]{:S(2)}) copy-start(f32[4,27648]{1,0:T(4,128)S(1)} %reshape.19) | copy-start | bytes 1327108
Sparse Core Ops, SparseCore 0:
  11.0 162.2 all-gather.2
  201.9 16.0 reduce-scatter.3
where the time goes:
time: 227 us; the launch traced here: 226 us
  Pallas kernels  91.1 us (40%)
  waiting for transfers between devices  84.7 us (37%)
  local copies, waits for them, and re-layouts  21.7 us (10%)
  between operations  14.1 us (6%)
  matrix products  13.6 us (6%)
    pallas_call x1, Pallas kernels, solve(): pl.pallas_call(functools.partial(solve_kernel, ng), out_shape=jax.ShapeDt...  91.1 us
    all_gather x1, waiting for transfers between devices, on_device(): lax.all_gather(orbitals, 'band', axis=0, tiled=True)  67.8 us
    unnamed x3, waiting for transfers between devices  16.9 us
    unnamed x5, local copies, waits for them, and re-layouts  16.2 us
    dot_general x1, matrix products, on_device(): lax.dot_general(lax.all_gather(orbitals, 'band', axis=0, tiled=True), vec...  13.6 us
  transfers between devices with their start and end apart: 2, of which 2 were waited for; matrix products, arithmetic and copies ran while one was open for 3% of the time, Pallas kernels for 40%

commit v1 on v0

--- a/solution.py
+++ b/solution.py
@@ -136,28 +136,28 @@
         return remote(src, buf.at[blk, slot], ssem.at[blk, lane], rsem.at[blk, slot], (band, target))
 
     barrier = pltpu.get_barrier_semaphore()
-    for device in ((band, sib), (band, cross), (band, far), (above, me), (below, me)):
+    for device in ((band, sib), (band, cross), (band, far), (above, cross), (below, cross)):
         pl.semaphore_signal(barrier, inc=1, device_id=device, device_id_type=mesh_id)
     pl.semaphore_wait(barrier, 5)
 
     share(0, 1, me, own_ref, cross).start()
     share(0, 0, me, own_ref, sib).start()
-    remote(own_ref, buf.at[1, me], nsem.at[0], rsem.at[1, me], (above, me)).start()
-    remote(own_ref, buf.at[2, me], nsem.at[1], rsem.at[2, me], (below, me)).start()
+    remote(own_ref, buf.at[1, me], nsem.at[0], rsem.at[1, me], (above, cross)).start()
+    remote(own_ref, buf.at[2, me], nsem.at[1], rsem.at[2, me], (below, cross)).start()
     local = pltpu.make_async_copy(own_ref, buf.at[0, me], lsem)
     local.start()
 
     def arrived(blk, slot):
         share(blk, 0, slot, own_ref, sib).wait_recv()
 
-    def relay(blk):
+    def relay(blk, slot):
+        arrived(blk, slot)
+        share(blk, 2, slot, buf.at[blk, slot], sib).start()
+
+    def spread(blk):
         arrived(blk, cross)
-        share(blk, 2, cross, buf.at[blk, cross], sib).start()
-
-    def spread(blk):
-        arrived(blk, me)
-        share(blk, 1, me, buf.at[blk, me], cross).start()
-        share(blk, 0, me, buf.at[blk, me], sib).start()
+        share(blk, 1, cross, buf.at[blk, cross], cross).start()
+        share(blk, 0, cross, buf.at[blk, cross], sib).start()
 
     def ztrans(v):
         hi, lo = split(v)
@@ -167,28 +167,34 @@
         hi, lo = split(v)
         return mm(ty_ref[...], jnp.concatenate([hi, lo, hi], axis=0))
 
-    def slot_of(s):
-        return ((chip + s // 2) % 2) * 2 + (core + s % 2) % 2
+    def slot_of(blk, s):
+        turn = s // 2 + jnp.minimum(blk, 1)
+        return ((chip + turn) % 2) * 2 + (core + s % 2) % 2
 
     def amplitude(slot):
         hi, lo = split(buf[0, slot].reshape(planes * ng, width))
         amp[slot] = (mm(hi, sel_ref[me]) + mm(lo, sel_ref[me])).reshape(planes, ng, width)
 
     def forward(blk, s):
-        slot = slot_of(s)
-
-        @pl.when(s == 1)
-        def _():
-            arrived(blk, sib)
+        slot = slot_of(blk, s)
 
         @pl.when(jnp.logical_and(blk == 0, s == 2))
         def _():
-            relay(0)
+            relay(0, cross)
             spread(1)
 
-        @pl.when(s == 3)
-        def _():
-            arrived(blk, far)
+        @pl.when(jnp.logical_and(blk == 1, s == 2))
+        def _():
+            relay(1, me)
+            spread(2)
+
+        @pl.when(jnp.logical_and(blk == 2, s == 2))
+        def _():
+            relay(2, me)
+
+        @pl.when(s % 2 == 1)
+        def _():
+            arrived(blk, slot)
 
         @pl.when(blk == 0)
         def _():
@@ -264,14 +270,6 @@
         def _():
             local.wait()
 
-        @pl.when(blk > 0)
-        def _():
-            relay(blk)
-
-        @pl.when(blk == 1)
-        def _():
-            spread(2)
-
         def fwd(s, _):
             forward(blk, s)
             return 0
@@ -298,8 +296,8 @@
     for blk in range(3):
         for lane, target in ((0, sib), (1, cross), (2, sib)):
             share(blk, lane, me, own_ref, target).wait_send()
-    remote(own_ref, buf.at[1, me], nsem.at[0], rsem.at[1, me], (above, me)).wait_send()
-    remote(own_ref, buf.at[2, me], nsem.at[1], rsem.at[2, me], (below, me)).wait_send()
+    remote(own_ref, buf.at[1, me], nsem.at[0], rsem.at[1, me], (above, cross)).wait_send()
+    remote(own_ref, buf.at[2, me], nsem.at[1], rsem.at[2, me], (below, cross)).wait_send()
 
 
 def lane_tables(ng, bands):
@@ -351,6 +349,140 @@
     )(own, *[jnp.asarray(c) for c in consts])
 
 
+def margin_kernel(count, size, orb_ref, vec_ref, o_ref, ro, rv, xo, xv, gs, gr, ps, pr,
+                  so, sv, qo, qv, sg, qg, sp, qp):
+    bands, ncell = orb_ref.shape[0], orb_ref.shape[1] * lax.axis_size("grid")
+    me, band, nband = lax.axis_index("grid"), lax.axis_index("band"), lax.axis_size("band")
+    chip, core = me // 2, me % 2
+    sib = chip * 2 + (1 - core)
+    cross = (1 - chip) * 2 + core
+    far = (1 - chip) * 2 + (1 - core)
+    mesh_id = pl.DeviceIdType.MESH
+
+    def remote(src, dst, send, recv_sem, device):
+        return pltpu.make_async_remote_copy(
+            src_ref=src, dst_ref=dst, send_sem=send, recv_sem=recv_sem,
+            device_id=device, device_id_type=mesh_id,
+        )
+
+    def each(n, body):
+        def step(k, _):
+            body(k)
+            return 0
+
+        lax.fori_loop(0, n, step, 0)
+
+    barrier = pltpu.get_barrier_semaphore()
+    each(nband, lambda b: pl.semaphore_signal(barrier, inc=1, device_id=(b, cross), device_id_type=mesh_id))
+    for other in (sib, far):
+        pl.semaphore_signal(barrier, inc=1, device_id=(band, other), device_id_type=mesh_id)
+    pl.semaphore_wait(barrier, nband + 2)
+
+    def part(src, dst, send, recv_sem, c):
+        cells = pl.ds(pl.multiple_of(c * size, 128), size)
+        return remote(src.at[:, cells], dst.at[band], send.at[c], recv_sem.at[band], (c, cross))
+
+    def target(k):
+        return (band + k) % count
+
+    each(count, lambda k: part(orb_ref, ro, so, qo, target(k)).start())
+    each(count, lambda k: part(vec_ref, rv, sv, qv, target(k)).start())
+
+    def term(b):
+        return remote(gs.at[b], gr.at[band], sg.at[b], qg.at[band], (b, cross))
+
+    @pl.when(band < count)
+    def _():
+        def take(src, dst, x, send, recv_sem):
+            def body(b):
+                cells = pl.ds(0, size)
+                remote(src.at[:, cells], dst.at[b], send.at[0], recv_sem.at[b], (b, cross)).wait_recv()
+
+            each(nband, body)
+
+            def rows(k):
+                for h in range(2):
+                    x[k, 4 * h : 4 * h + 4, :] = dst[2 * k + h]
+
+            each(nband // 2, rows)
+            return split(x[...].reshape(nband * bands, size))
+
+        oh, ol = take(orb_ref, ro, xo, so, qo)
+        vh, vl = take(vec_ref, rv, xv, sv, qv)
+
+        def nt(a, b):
+            return lax.dot_general(a, b, (((1,), (1,)), ((), ())), preferred_element_type=jnp.float32)
+
+        g = nt(vh, oh) + nt(vh, ol) + nt(vl, oh)
+        for b in range(nband):
+            gs[b] = g[4 * b : 4 * b + 4]
+        each(nband, lambda k: term((band + k) % nband).start())
+
+    def gather(c):
+        remote(gs.at[0], gr.at[c], sg.at[0], qg.at[c], (c, cross)).wait_recv()
+
+    each(count, gather)
+    total = gr[0]
+    for c in range(1, count):
+        total += gr[c]
+    ps[...] = total
+
+    def swap(slot):
+        return remote(ps, pr.at[me], sp.at[slot], qp.at[me], (band, slot))
+
+    for slot in (cross, far, sib):
+        swap(slot).start()
+    for slot in (cross, far, sib):
+        remote(ps, pr.at[slot], sp.at[slot], qp.at[slot], (band, slot)).wait()
+    pr[me] = total
+    full = (pr[0] + pr[1]) + (pr[2] + pr[3])
+    for k in range(4):
+        @pl.when(me == k)
+        def _():
+            width = o_ref.shape[1]
+            o_ref[...] = full[:, k * width : (k + 1) * width] * (1.0 / ncell)
+
+    each(count, lambda k: part(orb_ref, ro, so, qo, k).wait_send())
+    each(count, lambda k: part(vec_ref, rv, sv, qv, k).wait_send())
+
+    @pl.when(band < count)
+    def _():
+        each(nband, lambda k: term(k).wait_send())
+
+
+def chunking(local, nband):
+    tiles = local // 128
+    per = next(p for p in range(1, tiles + 1) if tiles % p == 0 and tiles // p <= nband)
+    return tiles // per, per * 128
+
+
+def margin_of(orbitals, vectors):
+    bands, local = orbitals.shape
+    nband, groups = lax.axis_size("band"), lax.axis_size("grid")
+    count, size = chunking(local, nband)
+    f32, dma = jnp.float32, pltpu.SemaphoreType.DMA
+    out = pl.pallas_call(
+        functools.partial(margin_kernel, count, size),
+        out_shape=jax.ShapeDtypeStruct((bands, nband * bands // groups), f32),
+        in_specs=[pl.BlockSpec(memory_space=pltpu.VMEM)] * 2,
+        out_specs=pl.BlockSpec(memory_space=pltpu.VMEM),
+        scratch_shapes=[
+            pltpu.VMEM((nband, bands, size), f32), pltpu.VMEM((nband, bands, size), f32),
+            pltpu.VMEM((nband // 2, 8, size), f32), pltpu.VMEM((nband // 2, 8, size), f32),
+            pltpu.VMEM((nband, bands, nband * bands), f32), pltpu.VMEM((count, bands, nband * bands), f32),
+            pltpu.VMEM((bands, nband * bands), f32), pltpu.VMEM((groups, bands, nband * bands), f32),
+            dma((count,)), dma((count,)), dma((nband,)), dma((nband,)),
+            dma((nband,)), dma((count,)), dma((groups,)), dma((groups,)),
+        ],
+        compiler_params=pltpu.CompilerParams(
+            vmem_limit_bytes=24 * 1024 * 1024, collective_id=1, has_side_effects=True
+        ),
+        cost_estimate=pl.CostEstimate(flops=10**9, bytes_accessed=10**6, transcendentals=0),
+        name="margin",
+    )(orbitals, vectors)
+    return out.T
+
+
 def on_device(orbitals):
     groups = lax.axis_size("grid")
     bands, local = orbitals.shape
@@ -363,17 +495,7 @@
     out = solve(own, bands, groups)
     vec = out[..., : 2 * ng].reshape(groups, planes, ng, 2, ng).transpose(0, 3, 1, 2, 4)
     vectors = vec.reshape(bands, local)
-    terms = (
-        lax.dot_general(
-            lax.all_gather(orbitals, "band", axis=0, tiled=True),
-            vectors,
-            (((1,), (1,)), ((), ())),
-            precision=lax.Precision.HIGHEST,
-            preferred_element_type=jnp.float32,
-        )
-        / ncell
-    )
-    margin = lax.psum_scatter(terms, "grid", scatter_dimension=0, tiled=True)
+    margin = margin_of(orbitals, vectors)
     return (vectors, margin)
 
 

time: 227 us -> 95.8 us (0.42)
  waiting for transfers between devices: 84.7 us -> 0 us
  local copies, waits for them, and re-layouts: 21.7 us -> 6.31 us
  matrix products: 13.6 us -> 0 us
  between operations: 14.1 us -> 0.71 us
  Pallas kernels: 91.1 us -> 87.4 us
    all_gather x1 -> x0, waiting for transfers between devices: 67.8 us -> none  [on_device(): lax.all_gather(orbitals, 'band', axis=0, tiled=True)]
    pallas_call x1, Pallas kernels: 91.1 us -> 57.8 us  [solve(): pl.pallas_call(functools.partial(solve_kernel, ng), out_shape=jax.ShapeDt...]
    pallas_call x0 -> x1, Pallas kernels: none -> 29.6 us  [margin_of(): pl.pallas_call(functools.partial(margin_kernel, count, size), out_shape=j...]
    unnamed x3 -> x0, waiting for transfers between devices: 16.9 us -> none
    unnamed x5, local copies, waits for them, and re-layouts: 16.2 us -> 0.79 us
    dot_general x1 -> x0, matrix products: 13.6 us -> none  [on_device(): lax.dot_general(lax.all_gather(orbitals, 'band', axis=0, tiled=True), vec...]
  transfers between devices with their start and end apart: 2 -> 0, of which waited for: 2 -> 0; matrix products, arithmetic and copies ran while one was open for 3% -> 0% of each run, Pallas kernels for 40% -> 0%
where the time goes in v1:
time: 95.8 us; the launch traced here: 95.3 us
  Pallas kernels  87.4 us (91%)
  local copies, waits for them, and re-layouts  6.31 us (7%)
    pallas_call x1, Pallas kernels, solve(): pl.pallas_call(functools.partial(solve_kernel, ng), out_shape=jax.ShapeDt...  57.8 us
    pallas_call x1, Pallas kernels, margin_of(): pl.pallas_call(functools.partial(margin_kernel, count, size), out_shape=j...  29.6 us
    reshape x3, local copies, waits for them, and re-layouts, on_device(): orbitals.reshape(bands, 2, planes, ng, ng).transpose(2, 3, 1, 0, 4)  2.85 us

profile of v1, /device:TPU:1, one launch (start us, length us, event | category | flops | bytes accessed | tf_op | source)
XLA Modules:
  0.0 95.3 jit_solution(13170486877027251342)
XLA Ops:
  0.6 1.6 %reshape.16 = f32[4,2,6,48,48]{4,3,2,1,0:T(8,128)S(1)} reshape(f32[4,27648]{1,0:T(4,128)} %orb_ref.1) | data formatting | bytes 884736 | tf_op jit(solution)/shard_map/reshape | solution.py:493
  2.2 0.8 copy.15
  3.0 0.5 reshape.17
  3.6 0.9 pad_maximum_fusion.own_ref
  4.4 57.8 %solve.1 = f32[4,6,48,128]{3,2,1,0:T(8,128)} custom-call(f32[6,48,384]{2,1,0:T(8,128)} %pad_maximum_fusion.own_ref, f32[25,48,128]{2,1,0:T(8,128)} %constant.14.clone.k1_ref, f32[25,24,128]{2,1,0:T(8,128)} %constant.15.clone.k2_ref, bf16[384,384]{1,0:T(8,128)(2,1)} %constant.16.clone.zh_ref, bf16[384,384]{1,0:T(8,128)(2,1)} %constant.17.clone.zl_ref, ...), custom_call_target="tpu_custom_call" | custom-call | flops 99999997952 | bytes 10000000 | tf_op jit(solution)/shard_map/solve/pallas_call | solution.py:334
  62.2 1.7 %reshape.18 = f32[4,6,48,2,48]{4,3,2,1,0:T(2,128)S(1)} reshape(f32[4,6,48,96]{3,2,1,0:T(8,128)} %bitcast.25) | data formatting | bytes 884736 | tf_op jit(solution)/shard_map/reshape | solution.py:496
  64.0 0.1 copy.14
  64.1 0.0 copy-start
  64.1 0.8 reshape.19.vec_ref
  64.9 0.2 copy-done
  65.1 0.0 copy-start.1
  65.1 29.6 %margin.1 = f32[4,32]{1,0:T(4,128)S(1)} custom-call(f32[4,27648]{1,0:T(4,128)S(1)} %copy-done, f32[4,27648]{1,0:T(4,128)S(1)} %reshape.19.vec_ref), custom_call_target="tpu_custom_call" | custom-call | flops 1000000000 | bytes 1000000 | tf_op jit(solution)/shard_map/margin/pallas_call | solution.py:464
  94.7 0.0 copy-done.1
  94.7 0.6 copy.17
  (2 shorter events, 0.0 us)
Async XLA Ops:
  64.1 1.0 %copy-start = (f32[4,27648]{1,0:T(4,128)S(1)}, f32[4,27648]{1,0:T(4,128)}, u32[]{:S(2)}) copy-start(f32[4,27648]{1,0:T(4,128)} %orb_ref.1) | copy-start | bytes 1327108
  65.1 29.6 %copy-start.1 = (f32[4,27648]{1,0:T(4,128)}, f32[4,27648]{1,0:T(4,128)S(1)}, u32[]{:S(2)}) copy-start(f32[4,27648]{1,0:T(4,128)S(1)} %reshape.19.vec_ref) | copy-start | bytes 1327108

commit v2 on v1

v2 whole, which is shorter than its diff:
```python
import functools

import jax
import jax.numpy as jnp
import numpy as np
from jax import lax
from jax.experimental import pallas as pl
from jax.experimental.pallas import tpu as pltpu
from jax.sharding import PartitionSpec as P


PTS = 6


def freq_order(ng):
    step = ng // PTS
    low = np.arange(step) * PTS
    out = [low, low + 3]
    for k in (1, 2):
        out += [low + k, ng - low - k]
    return np.concatenate(out)


def kernel_values(ng):
    freqs = ((np.arange(ng) + ng // 2) % ng - ng // 2).astype(np.float32)
    fy = freqs[freq_order(ng)]
    sq = freqs[:, None, None] ** 2 + fy[None, :, None] ** 2 + freqs[None, None, :] ** 2
    safe = np.where(sq > 0, sq, np.float32(1.0))
    return np.where(sq > 0, 40.0 * (1.0 - np.exp(-sq / 16.0)) / safe, 0.0)


def cas(ang):
    return np.cos(ang) + np.sin(ang)


def hartley(ng):
    k = np.arange(ng)
    return cas((k[:, None] * k[None, :] % ng) * (2.0 * np.pi / ng))


def mixers(ng):
    step = ng // PTS
    s, k2 = np.arange(step)[:, None], np.arange(step)[None, :]
    out = []
    for k1 in (0, 3, 1, 2):
        ang = s * (k1 + PTS * k2) * (2.0 * np.pi / ng)
        p, m = cas(ang), cas(-ang)
        out.append(p if k1 in (0, 3) else np.block([[p, m], [m, -p]]))
    return out


def mixer_rows(ng):
    step = ng // PTS
    fwd, inv = [], []
    for mat in mixers(ng):
        for rows, keep in ((mat, fwd), (mat.T, inv)):
            wide = np.zeros((rows.shape[0], 2 * step))
            wide[:, : rows.shape[1]] = rows
            keep.append(np.repeat(wide, ng, axis=1))
    return np.stack([np.concatenate(fwd), np.concatenate(inv)])


def split_const(table):
    table = np.asarray(table, np.float32)
    hi = table.astype(jnp.bfloat16)
    lo = (table - hi.astype(np.float32)).astype(jnp.bfloat16)
    return hi, lo


def split(v):
    hi = v.astype(jnp.bfloat16)
    lo = (v - hi.astype(jnp.float32)).astype(jnp.bfloat16)
    return hi, lo


def mm(a, b):
    return jnp.dot(a, b, preferred_element_type=jnp.float32)


def solve_kernel(ng, own_ref, kt_ref, hz_ref, mix_ref, xh_ref, xl_ref, o_ref,
                 buf, amp, acc, ch, cl, zh, zl, cb, wh, wl, kx, vec, recv,
                 rsem, ssem, nsem, osem, orsem, lsem):
    pts, rows, width = own_ref.shape
    bands, step = 4, ng // PTS
    xs = rows // bands
    total = pts * width
    me = lax.axis_index("grid")
    band, nband = lax.axis_index("band"), lax.axis_size("band")
    chip, core = me // 2, me % 2
    sib = chip * 2 + (1 - core)
    cross = (1 - chip) * 2 + core
    far = (1 - chip) * 2 + (1 - core)
    above, below = (band + 1) % nband, (band + nband - 1) % nband
    mesh_id = pl.DeviceIdType.MESH
    root = np.float32(np.sqrt(0.75))

    def remote(src, dst, send, recv_sem, device):
        return pltpu.make_async_remote_copy(
            src_ref=src, dst_ref=dst, send_sem=send, recv_sem=recv_sem,
            device_id=device, device_id_type=mesh_id,
        )

    def share(blk, lane, slot, src, target):
        return remote(src, buf.at[blk, slot], ssem.at[blk, lane], rsem.at[blk, slot], (band, target))

    def each(n, body):
        def one(k, _):
            body(k)
            return 0

        lax.fori_loop(0, n, one, 0)

    barrier = pltpu.get_barrier_semaphore()
    for device in ((band, sib), (band, cross), (band, far), (above, cross), (below, cross)):
        pl.semaphore_signal(barrier, inc=1, device_id=device, device_id_type=mesh_id)
    pl.semaphore_wait(barrier, 5)

    share(0, 1, me, own_ref, cross).start()
    share(0, 0, me, own_ref, sib).start()
    remote(own_ref, buf.at[1, me], nsem.at[0], rsem.at[1, me], (above, cross)).start()
    remote(own_ref, buf.at[2, me], nsem.at[1], rsem.at[2, me], (below, cross)).start()
    local = pltpu.make_async_copy(own_ref, buf.at[0, me], lsem)
    local.start()

    def weights(first, last, cols):
        def one(u, _):
            at = pl.ds(pl.multiple_of(u * ng, 16), ng)
            for d in range(2):
                hi, lo = split(hz_ref[:, :cols] * mix_ref[d, pl.ds(u, 1), :cols])
                wh[d, at, :cols] = hi
                wl[d, at, :cols] = lo
            return 0

        lax.fori_loop(first, last, one, 0)

    weights(0, 2 * step, width)
    weights(2 * step, PTS * step, 2 * width)

    def spread_rows(t):
        upper = lax.broadcasted_iota(jnp.int32, (8, total), 0) < 4
        a = jnp.broadcast_to(kt_ref[pl.ds(2 * t, 1), :], (8, total))
        b = jnp.broadcast_to(kt_ref[pl.ds(2 * t + 1, 1), :], (8, total))
        kx[pl.ds(pl.multiple_of(8 * t, 8), 8), :] = jnp.where(upper, a, b)

    each(ng // 2, spread_rows)

    def arrived(blk, slot):
        share(blk, 0, slot, own_ref, sib).wait_recv()

    def relay(blk, slot):
        arrived(blk, slot)
        share(blk, 2, slot, buf.at[blk, slot], sib).start()

    def spread(blk):
        arrived(blk, cross)
        share(blk, 1, cross, buf.at[blk, cross], cross).start()
        share(blk, 0, cross, buf.at[blk, cross], sib).start()

    def slot_of(blk, s):
        turn = s // 2 + jnp.minimum(blk, 1)
        return ((chip + turn) % 2) * 2 + (core + s % 2) % 2

    def amplitude(slot):
        sub = lax.broadcasted_iota(jnp.int32, (8, 128), 0)
        pick = sub // bands * bands + me

        def one(r):
            for q in range(rows // 8):
                for j in range(width // 128):
                    at = (slot, r, pl.ds(8 * q, 8), pl.ds(128 * j, 128))
                    amp[at] = jnp.take_along_axis(buf[(0,) + at], pick, axis=0)

        each(pts, one)

    def pieces():
        for q in range(rows // 16):
            for j in range(width // 128):
                yield q, j

    def forward(blk, s):
        slot = slot_of(blk, s)

        @pl.when(jnp.logical_and(blk == 0, s == 2))
        def _():
            relay(0, cross)
            spread(1)

        @pl.when(jnp.logical_and(blk == 1, s == 2))
        def _():
            relay(1, me)
            spread(2)

        @pl.when(jnp.logical_and(blk == 2, s == 2))
        def _():
            relay(2, me)

        @pl.when(s % 2 == 1)
        def _():
            arrived(blk, slot)

        @pl.when(blk == 0)
        def _():
            amplitude(slot)

        for q, j in pieces():
            at = (pl.ds(16 * q, 16), pl.ds(128 * j, 128))
            f = [amp[(slot, r) + at] * buf[(blk, slot, r) + at] for r in range(PTS)]
            sa, sb, sc = f[0] + f[3], f[1] + f[4], f[2] + f[5]
            da, db, dc = f[0] - f[3], f[1] - f[4], f[2] - f[5]
            even, odd = sb + sc, db - dc
            comps = (sa + even, da - odd, da + 0.5 * odd, root * (db + dc), sa - 0.5 * even, root * (sb - sc))
            to = pl.ds(pl.multiple_of(slot * rows + 16 * q, 16), 16)
            for c, v in enumerate(comps):
                hi, lo = split(v)
                ch[to, c * width + 128 * j : c * width + 128 * j + 128] = hi
                cl[to, c * width + 128 * j : c * width + 128 * j + 128] = lo

    groups = ((0, 1), (1, 1), (2, 2), (4, 2))

    def planar(d, ah, al, emit):
        for first, count in groups:
            lo, size = first * width, count * width
            for n in range(0, size, 256):
                w = min(256, size - n)
                a, b = ah[:, lo : lo + size], al[:, lo : lo + size]
                g, h = wh[d, lo : lo + size, n : n + w], wl[d, lo : lo + size, n : n + w]
                emit(lo + n, w, mm(a, g) + mm(b, g) + mm(a, h))

    def keep_split(at, w, v):
        zh[:, at : at + w], zl[:, at : at + w] = split(v)

    def keep(at, w, v):
        cb[:, at : at + w] = v

    def xpass(h, l):
        return mm(xh_ref[...], h) + mm(xh_ref[...], l) + mm(xl_ref[...], h)

    def xconv():
        for n in range(0, total, 256):
            h, l = split(xpass(zh[:, n : n + 256], zl[:, n : n + 256]) * kx[:, n : n + 256])
            zh[:, n : n + 256], zl[:, n : n + 256] = split(xpass(h, l))

    def push(slot):
        return remote(vec.at[slot], recv.at[me], osem.at[slot], orsem.at[me], (band, slot))

    def inverse(blk, s):
        slot = ((chip + 1 - s // 2) % 2) * 2 + (core + s % 2 + s // 2) % 2
        fresh = blk == 0
        for q, j in pieces():
            to = pl.ds(pl.multiple_of(slot * rows + 16 * q, 16), 16)
            c0, c3, c1, s1, c2, s2 = [cb[to, c * width + 128 * j : c * width + 128 * j + 128] for c in range(PTS)]
            ea, eb, oa, ob = c0 - 0.5 * c2, root * s2, c3 - 0.5 * c1, root * s1
            even = (c0 + c2, ea + eb, ea - eb)
            odd = (c3 + c1, ob - oa, oa + ob)
            for r in range(PTS):
                v = even[r % 3] + odd[r % 3] if r < 3 else even[r % 3] - odd[r % 3]
                w = v * buf[blk, slot, r, 16 * q : 16 * q + 16, 128 * j : 128 * j + 128]
                at = (slot, j, pl.ds(rows * r + 16 * q, 16))
                acc[at] = jnp.where(fresh, w, acc[at] + w)

        @pl.when(blk == 2)
        def _():
            for j in range(width // 128):
                t = [acc[slot, j, pl.ds(b, pts * xs, stride=bands), :] for b in range(bands)]
                vec[slot, :, 128 * j : 128 * j + 128] = -((t[0] + t[1]) + (t[2] + t[3]))

            @pl.when(s < 3)
            def _():
                push(slot).start()

    def block(blk):
        @pl.when(blk == 0)
        def _():
            local.wait()

        each(4, lambda s: forward(blk, s))
        planar(0, ch, cl, keep_split)
        xconv()
        planar(1, zh, zl, keep)
        each(4, lambda s: inverse(blk, s))

    each(3, block)

    def place(slot, src):
        for r in range(pts):
            for j in range(width // 128):
                piece = src[xs * r : xs * r + xs, 128 * j : 128 * j + 128]
                o_ref[pl.ds(bands * (width // 128 * r + j) + slot, xs, stride=pts * width // 128 * bands), :] = piece

    recv[me] = vec[me]
    for slot in (sib, cross, far):
        remote(vec.at[slot], recv.at[slot], osem.at[slot], orsem.at[slot], (band, slot)).wait()
    for k in range(4):
        place(k, recv[k])
    for blk in range(3):
        for lane, target in ((0, sib), (1, cross), (2, sib)):
            share(blk, lane, me, own_ref, target).wait_send()
    remote(own_ref, buf.at[1, me], nsem.at[0], rsem.at[1, me], (above, cross)).wait_send()
    remote(own_ref, buf.at[2, me], nsem.at[1], rsem.at[2, me], (below, cross)).wait_send()


def solve(own, bands, groups, ng):
    pts, rows, width = own.shape
    step = ng // PTS
    total = pts * width
    xh, xl = split_const(np.kron(hartley(ng), np.eye(bands)))
    hz = np.tile(hartley(ng), (1, 2 * step)).astype(np.float32)
    kt = (kernel_values(ng).astype(np.float32) / np.float32(ng**3)).reshape(ng, total)
    consts = [kt, hz, mixer_rows(ng).astype(np.float32), xh, xl]
    full = (groups, pts, rows, width)
    f32, bf16, dma = jnp.float32, jnp.bfloat16, pltpu.SemaphoreType.DMA
    tall = groups * rows
    xs = rows // bands
    return pl.pallas_call(
        functools.partial(solve_kernel, ng),
        out_shape=jax.ShapeDtypeStruct((pts * rows * width // 128, 128), f32),
        in_specs=[pl.BlockSpec(memory_space=pltpu.VMEM)] * 6,
        out_specs=pl.BlockSpec(memory_space=pltpu.VMEM),
        scratch_shapes=[
            pltpu.VMEM((3,) + full, f32), pltpu.VMEM(full, f32),
            pltpu.VMEM((groups, width // 128, pts * rows, 128), f32),
            pltpu.VMEM((tall, total), bf16), pltpu.VMEM((tall, total), bf16),
            pltpu.VMEM((tall, total), bf16), pltpu.VMEM((tall, total), bf16),
            pltpu.VMEM((tall, total), f32),
            pltpu.VMEM((2, total, 2 * width), bf16), pltpu.VMEM((2, total, 2 * width), bf16),
            pltpu.VMEM((tall, total), f32),
            pltpu.VMEM((groups, pts * xs, width), f32), pltpu.VMEM((groups, pts * xs, width), f32),
            dma((3, groups)), dma((3, 3)), dma((2,)), dma((groups,)), dma((groups,)), dma(()),
        ],
        compiler_params=pltpu.CompilerParams(
            vmem_limit_bytes=56 * 1024 * 1024, collective_id=0, has_side_effects=True
        ),
        cost_estimate=pl.CostEstimate(flops=10**11, bytes_accessed=10**7, transcendentals=0),
        name="solve",
    )(own, *[jnp.asarray(c) for c in consts])


def margin_kernel(count, size, orb_ref, vec_ref, o_ref, ro, rv, xo, xv, gs, gr, ps, pr,
                  so, sv, qo, qv, sg, qg, sp, qp):
    bands, ncell = orb_ref.shape[0], orb_ref.shape[1] * lax.axis_size("grid")
    me, band, nband = lax.axis_index("grid"), lax.axis_index("band"), lax.axis_size("band")
    chip, core = me // 2, me % 2
    sib = chip * 2 + (1 - core)
    cross = (1 - chip) * 2 + core
    far = (1 - chip) * 2 + (1 - core)
    mesh_id = pl.DeviceIdType.MESH

    def remote(src, dst, send, recv_sem, device):
        return pltpu.make_async_remote_copy(
            src_ref=src, dst_ref=dst, send_sem=send, recv_sem=recv_sem,
            device_id=device, device_id_type=mesh_id,
        )

    def each(n, body):
        def step(k, _):
            body(k)
            return 0

        lax.fori_loop(0, n, step, 0)

    barrier = pltpu.get_barrier_semaphore()
    each(nband, lambda b: pl.semaphore_signal(barrier, inc=1, device_id=(b, cross), device_id_type=mesh_id))
    for other in (sib, far):
        pl.semaphore_signal(barrier, inc=1, device_id=(band, other), device_id_type=mesh_id)
    pl.semaphore_wait(barrier, nband + 2)

    def part(src, dst, send, recv_sem, c):
        cells = pl.ds(pl.multiple_of(c * size, 128), size)
        return remote(src.at[:, cells], dst.at[band], send.at[c], recv_sem.at[band], (c, cross))

    def target(k):
        return (band + k) % count

    each(count, lambda k: part(orb_ref, ro, so, qo, target(k)).start())
    each(count, lambda k: part(vec_ref, rv, sv, qv, target(k)).start())

    def term(b):
        return remote(gs.at[b], gr.at[band], sg.at[b], qg.at[band], (b, cross))

    @pl.when(band < count)
    def _():
        def take(src, dst, x, send, recv_sem):
            def body(b):
                cells = pl.ds(0, size)
                remote(src.at[:, cells], dst.at[b], send.at[0], recv_sem.at[b], (b, cross)).wait_recv()

            each(nband, body)

            def rows(k):
                for h in range(2):
                    x[k, 4 * h : 4 * h + 4, :] = dst[2 * k + h]

            each(nband // 2, rows)
            return split(x[...].reshape(nband * bands, size))

        oh, ol = take(orb_ref, ro, xo, so, qo)
        vh, vl = take(vec_ref, rv, xv, sv, qv)

        def nt(a, b):
            return lax.dot_general(a, b, (((1,), (1,)), ((), ())), preferred_element_type=jnp.float32)

        g = nt(vh, oh) + nt(vh, ol) + nt(vl, oh)
        for b in range(nband):
            gs[b] = g[4 * b : 4 * b + 4]
        each(nband, lambda k: term((band + k) % nband).start())

    def gather(c):
        remote(gs.at[0], gr.at[c], sg.at[0], qg.at[c], (c, cross)).wait_recv()

    each(count, gather)
    total = gr[0]
    for c in range(1, count):
        total += gr[c]
    ps[...] = total

    def swap(slot):
        return remote(ps, pr.at[me], sp.at[slot], qp.at[me], (band, slot))

    for slot in (cross, far, sib):
        swap(slot).start()
    for slot in (cross, far, sib):
        remote(ps, pr.at[slot], sp.at[slot], qp.at[slot], (band, slot)).wait()
    pr[me] = total
    full = (pr[0] + pr[1]) + (pr[2] + pr[3])
    for k in range(4):
        @pl.when(me == k)
        def _():
            width = o_ref.shape[1]
            o_ref[...] = full[:, k * width : (k + 1) * width] * (1.0 / ncell)

    each(count, lambda k: part(orb_ref, ro, so, qo, k).wait_send())
    each(count, lambda k: part(vec_ref, rv, sv, qv, k).wait_send())

    @pl.when(band < count)
    def _():
        each(nband, lambda k: term(k).wait_send())


def chunking(local, nband):
    tiles = local // 128
    per = next(p for p in range(1, tiles + 1) if tiles % p == 0 and tiles // p <= nband)
    return tiles // per, per * 128


def margin_of(orbitals, vectors):
    bands, local = orbitals.shape
    nband, groups = lax.axis_size("band"), lax.axis_size("grid")
    count, size = chunking(local, nband)
    f32, dma = jnp.float32, pltpu.SemaphoreType.DMA
    out = pl.pallas_call(
        functools.partial(margin_kernel, count, size),
        out_shape=jax.ShapeDtypeStruct((bands, nband * bands // groups), f32),
        in_specs=[pl.BlockSpec(memory_space=pltpu.VMEM)] * 2,
        out_specs=pl.BlockSpec(memory_space=pltpu.VMEM),
        scratch_shapes=[
            pltpu.VMEM((nband, bands, size), f32), pltpu.VMEM((nband, bands, size), f32),
            pltpu.VMEM((nband // 2, 8, size), f32), pltpu.VMEM((nband // 2, 8, size), f32),
            pltpu.VMEM((nband, bands, nband * bands), f32), pltpu.VMEM((count, bands, nband * bands), f32),
            pltpu.VMEM((bands, nband * bands), f32), pltpu.VMEM((groups, bands, nband * bands), f32),
            dma((count,)), dma((count,)), dma((nband,)), dma((nband,)),
            dma((nband,)), dma((count,)), dma((groups,)), dma((groups,)),
        ],
        compiler_params=pltpu.CompilerParams(
            vmem_limit_bytes=24 * 1024 * 1024, collective_id=1, has_side_effects=True
        ),
        cost_estimate=pl.CostEstimate(flops=10**9, bytes_accessed=10**6, transcendentals=0),
        name="margin",
    )(orbitals, vectors)
    return out.T


def on_device(orbitals):
    groups = lax.axis_size("grid")
    bands, local = orbitals.shape
    ncell = local * groups
    ng = round(ncell ** (1 / 3))
    xs, wide = local // (ng * ng), ng * ng // PTS
    t = orbitals.reshape(bands, xs, PTS, wide // 128, 128).transpose(2, 1, 0, 3, 4)
    out = solve(t.reshape(PTS, xs * bands, wide), bands, groups, ng)
    vectors = out.reshape(local // 128, bands, 128).transpose(1, 0, 2).reshape(bands, local)
    margin = margin_of(orbitals, vectors)
    return (vectors, margin)


def solution(mesh):
    return jax.shard_map(
        on_device,
        mesh=mesh,
        in_specs=(P("band", "grid"),),
        out_specs=(P("band", "grid"), P("grid", "band")),
        check_vma=False,
    )
```

time: 95.8 us -> 92.3 us (0.963)
  Pallas kernels: 87.4 us -> 86.2 us
  local copies, waits for them, and re-layouts: 6.31 us -> 5.14 us
    reshape x6 -> x3, local copies, waits for them, and re-layouts: 5.48 us -> 3.45 us  [the longest x1 1.41 us: on_device(): orbitals.reshape(bands, xs, PTS, wide // 128, 128).transpose(2, 1, 0, 3, 4)]
    pallas_call x1, Pallas kernels: 57.8 us -> 56.6 us  [solve(): pl.pallas_call(functools.partial(solve_kernel, ng), out_shape=jax.ShapeDt...]
where the time goes in v2:
time: 92.3 us; the launch traced here: 92.1 us
  Pallas kernels  86.2 us (93%)
  local copies, waits for them, and re-layouts  5.14 us (6%)
    pallas_call x1, Pallas kernels, solve(): pl.pallas_call(functools.partial(solve_kernel, ng), out_shape=jax.ShapeDt...  56.6 us
    pallas_call x1, Pallas kernels, margin_of(): pl.pallas_call(functools.partial(margin_kernel, count, size), out_shape=j...  29.7 us

profile of v2, /device:TPU:1, one launch (start us, length us, event | category | flops | bytes accessed | tf_op | source)
XLA Modules:
  0.0 92.1 jit_solution(12497993186543503850)
XLA Ops:
  0.6 1.4 %reshape.16 = f32[4,12,6,3,128]{4,3,2,1,0:T(4,128)S(1)} reshape(f32[4,27648]{1,0:T(4,128)} %orb_ref.1) | data formatting | bytes 884736 | tf_op jit(solution)/shard_map/reshape | solution.py:478
  2.0 0.1 copy.10
  2.2 1.0 %reshape.17.own_ref = f32[6,48,384]{2,1,0:T(8,128)} reshape(f32[6,12,4,3,128]{4,3,2,1,0:T(4,128)S(1)} %copy.10) | data formatting | bytes 884736 | tf_op jit(solution)/shard_map/reshape | solution.py:479
  3.2 56.6 %solve.1 = f32[864,128]{1,0:T(8,128)} custom-call(f32[6,48,384]{2,1,0:T(8,128)} %reshape.17.own_ref, f32[48,2304]{1,0:T(8,128)} %constant.10.clone.kt_ref, f32[48,768]{1,0:T(8,128)} %constant.11.clone.hz_ref, f32[2,48,768]{2,1,0:T(8,128)} %constant.12.clone.mix_ref, bf16[192,192]{1,0:T(8,128)(2,1)} %constant.13.clone.xh_ref, ...), custom_call_target="tpu_custom_call" | custom-call | flops 99999997952 | bytes 10000000 | tf_op jit(solution)/shard_map/solve/pallas_call | solution.py:314
  59.7 1.0 %copy.16 = f32[216,4,128]{2,0,1:T(8,128)S(1)} copy(f32[216,4,128]{2,1,0:T(4,128)} %bitcast.15) | data formatting | bytes 884736 | tf_op jit(solution)/shard_map/reshape | solution.py:480
  60.8 0.0 copy-start.1
  60.8 0.1 copy.15
  60.9 0.0 copy-start
  60.9 0.9 copy-done.1
  61.8 29.7 %margin.1 = f32[4,32]{1,0:T(4,128)S(1)} custom-call(f32[4,27648]{1,0:T(4,128)S(1)} %copy-done.1, f32[4,27648]{1,0:T(4,128)S(1)} %bitcast.10), custom_call_target="tpu_custom_call" | custom-call | flops 1000000000 | bytes 1000000 | tf_op jit(solution)/shard_map/margin/pallas_call | solution.py:450
  91.5 0.0 copy-done
  91.5 0.6 copy.18
Async XLA Ops:
  60.8 1.0 %copy-start.1 = (f32[4,27648]{1,0:T(4,128)S(1)}, f32[4,27648]{1,0:T(4,128)}, u32[]{:S(2)}) copy-start(f32[4,27648]{1,0:T(4,128)} %orb_ref.1) | copy-start | bytes 1327108
  60.9 30.6 %copy-start = (f32[1,4,216,128]{3,1,2,0:T(4,128)}, f32[1,4,216,128]{3,1,2,0:T(4,128)S(1)}, u32[]{:S(2)}) copy-start(f32[1,4,216,128]{3,1,2,0:T(4,128)S(1)} %copy.15) | copy-start | bytes 1327108

commit v3 on v2

--- a/solution.py
+++ b/solution.py
@@ -77,10 +77,11 @@
     return jnp.dot(a, b, preferred_element_type=jnp.float32)
 
 
-def solve_kernel(ng, own_ref, kt_ref, hz_ref, mix_ref, xh_ref, xl_ref, o_ref,
+def solve_kernel(ng, count, orb_ref, kt_ref, hz_ref, mix_ref, xh_ref, xl_ref, o_ref, m_ref,
                  buf, amp, acc, ch, cl, zh, zl, cb, wh, wl, kx, vec, recv,
-                 rsem, ssem, nsem, osem, orsem, lsem):
-    pts, rows, width = own_ref.shape
+                 ro, rv, xo, xv, gs, gr, ps, pr,
+                 rsem, ssem, nsem, osem, orsem, so, sv, qo, qv, sg, qg, sp, qp):
+    pts, rows, width = buf.shape[2:]
     bands, step = 4, ng // PTS
     xs = rows // bands
     total = pts * width
@@ -110,17 +111,30 @@
 
         lax.fori_loop(0, n, one, 0)
 
+    own_ref = buf.at[0, me]
+
+    def lay_own(q):
+        for h in range(2):
+            for r in range(pts):
+                for j in range(width // 128):
+                    unit = ((2 * q + h) * pts + r) * (width // 128) + j
+                    piece = orb_ref[bands * unit : bands * unit + bands, :]
+                    at = (me, r, pl.ds(8 * q + 4 * h, bands), pl.ds(128 * j, 128))
+                    buf[(0,) + at] = piece
+
+    for q in range(xs // 2):
+        lay_own(q)
+
     barrier = pltpu.get_barrier_semaphore()
-    for device in ((band, sib), (band, cross), (band, far), (above, cross), (below, cross)):
-        pl.semaphore_signal(barrier, inc=1, device_id=device, device_id_type=mesh_id)
-    pl.semaphore_wait(barrier, 5)
+    each(nband, lambda b: pl.semaphore_signal(barrier, inc=1, device_id=(b, cross), device_id_type=mesh_id))
+    for other in (sib, far):
+        pl.semaphore_signal(barrier, inc=1, device_id=(band, other), device_id_type=mesh_id)
+    pl.semaphore_wait(barrier, nband + 2)
 
     share(0, 1, me, own_ref, cross).start()
     share(0, 0, me, own_ref, sib).start()
     remote(own_ref, buf.at[1, me], nsem.at[0], rsem.at[1, me], (above, cross)).start()
     remote(own_ref, buf.at[2, me], nsem.at[1], rsem.at[2, me], (below, cross)).start()
-    local = pltpu.make_async_copy(own_ref, buf.at[0, me], lsem)
-    local.start()
 
     def weights(first, last, cols):
         def one(u, _):
@@ -268,14 +282,80 @@
             def _():
                 push(slot).start()
 
+    size = orb_ref.shape[0] // count
+
+    def part(src, dst, send, recv_sem, c):
+        cells = pl.ds(pl.multiple_of(c * size, 8), size)
+        return remote(src.at[cells], dst.at[band], send.at[c], recv_sem.at[band], (c, cross))
+
+    def target(k):
+        return (band + k) % count
+
+    def term(b):
+        return remote(gs.at[b], gr.at[band], sg.at[b], qg.at[band], (b, cross))
+
+    def take(src, dst, x, send, recv_sem):
+        def body(b):
+            remote(src.at[pl.ds(0, size)], dst.at[b], send.at[0], recv_sem.at[b], (b, cross)).wait_recv()
+
+        each(nband, body)
+
+        def lay(k):
+            for h in range(2):
+                for t in range(size // bands):
+                    row = dst[2 * k + h, bands * t : bands * t + bands, :]
+                    x[k, 4 * h : 4 * h + 4, 128 * t : 128 * t + 128] = row
+
+        each(nband // 2, lay)
+
+    def nt(a, b):
+        return lax.dot_general(a, b, (((1,), (1,)), ((), ())), preferred_element_type=jnp.float32)
+
+    def swap(slot):
+        return remote(ps, pr.at[me], sp.at[slot], qp.at[me], (band, slot))
+
+    def margin():
+        wide = size // bands * 128
+
+        @pl.when(band < count)
+        def _():
+            take(orb_ref, ro, xo, so, qo)
+            oh, ol = split(xo[...].reshape(nband * bands, wide))
+            take(o_ref, rv, xv, sv, qv)
+            vh, vl = split(xv[...].reshape(nband * bands, wide))
+            g = nt(vh, oh) + nt(vh, ol) + nt(vl, oh)
+            for b in range(nband):
+                gs[b] = g[4 * b : 4 * b + 4]
+            each(nband, lambda k: term((band + k) % nband).start())
+
+        def gather(c):
+            remote(gs.at[0], gr.at[c], sg.at[0], qg.at[c], (c, cross)).wait_recv()
+
+        each(count, gather)
+        sums = gr[0]
+        for c in range(1, count):
+            sums += gr[c]
+        ps[...] = sums
+        for slot in (cross, far, sib):
+            swap(slot).start()
+        for slot in (cross, far, sib):
+            remote(ps, pr.at[slot], sp.at[slot], qp.at[slot], (band, slot)).wait()
+        pr[me] = sums
+        full = ((pr[0] + pr[1]) + (pr[2] + pr[3])) * (1.0 / ng**3)
+        for k in range(4):
+            @pl.when(me == k)
+            def _():
+                m_ref[...] = full[:, k * m_ref.shape[1] : (k + 1) * m_ref.shape[1]]
+
     def block(blk):
-        @pl.when(blk == 0)
-        def _():
-            local.wait()
-
         each(4, lambda s: forward(blk, s))
         planar(0, ch, cl, keep_split)
         xconv()
+
+        @pl.when(blk == 1)
+        def _():
+            each(count, lambda k: part(orb_ref, ro, so, qo, target(k)).start())
+
         planar(1, zh, zl, keep)
         each(4, lambda s: inverse(blk, s))
 
@@ -292,6 +372,15 @@
         remote(vec.at[slot], recv.at[slot], osem.at[slot], orsem.at[slot], (band, slot)).wait()
     for k in range(4):
         place(k, recv[k])
+    each(count, lambda k: part(o_ref, rv, sv, qv, target(k)).start())
+    margin()
+    each(count, lambda k: part(orb_ref, ro, so, qo, k).wait_send())
+    each(count, lambda k: part(o_ref, rv, sv, qv, k).wait_send())
+
+    @pl.when(band < count)
+    def _():
+        each(nband, lambda k: term(k).wait_send())
+
     for blk in range(3):
         for lane, target in ((0, sib), (1, cross), (2, sib)):
             share(blk, lane, me, own_ref, target).wait_send()
@@ -299,8 +388,9 @@
     remote(own_ref, buf.at[2, me], nsem.at[1], rsem.at[2, me], (below, cross)).wait_send()
 
 
-def solve(own, bands, groups, ng):
-    pts, rows, width = own.shape
+def solve(orb, bands, groups, nband, ng):
+    width = ng * ng // PTS
+    pts, rows = PTS, orb.shape[0] * 128 // (PTS * width)
     step = ng // PTS
     total = pts * width
     xh, xl = split_const(np.kron(hartley(ng), np.eye(bands)))
@@ -311,11 +401,14 @@
     f32, bf16, dma = jnp.float32, jnp.bfloat16, pltpu.SemaphoreType.DMA
     tall = groups * rows
     xs = rows // bands
+    count, wide = chunking(orb.shape[0] * 128 // bands, nband)
+    size, nall = wide * bands // 128, nband * bands
+    vmem = pl.BlockSpec(memory_space=pltpu.VMEM)
     return pl.pallas_call(
-        functools.partial(solve_kernel, ng),
-        out_shape=jax.ShapeDtypeStruct((pts * rows * width // 128, 128), f32),
-        in_specs=[pl.BlockSpec(memory_space=pltpu.VMEM)] * 6,
-        out_specs=pl.BlockSpec(memory_space=pltpu.VMEM),
+        functools.partial(solve_kernel, ng, count),
+        out_shape=[jax.ShapeDtypeStruct(orb.shape, f32), jax.ShapeDtypeStruct((bands, nall // groups), f32)],
+        in_specs=[vmem] * 6,
+        out_specs=[vmem] * 2,
         scratch_shapes=[
             pltpu.VMEM((3,) + full, f32), pltpu.VMEM(full, f32),
             pltpu.VMEM((groups, width // 128, pts * rows, 128), f32),
@@ -325,148 +418,26 @@
             pltpu.VMEM((2, total, 2 * width), bf16), pltpu.VMEM((2, total, 2 * width), bf16),
             pltpu.VMEM((tall, total), f32),
             pltpu.VMEM((groups, pts * xs, width), f32), pltpu.VMEM((groups, pts * xs, width), f32),
-            dma((3, groups)), dma((3, 3)), dma((2,)), dma((groups,)), dma((groups,)), dma(()),
+            pltpu.VMEM((nband, size, 128), f32), pltpu.VMEM((nband, size, 128), f32),
+            pltpu.VMEM((nband // 2, 8, wide), f32), pltpu.VMEM((nband // 2, 8, wide), f32),
+            pltpu.VMEM((nband, bands, nall), f32), pltpu.VMEM((count, bands, nall), f32),
+            pltpu.VMEM((bands, nall), f32), pltpu.VMEM((groups, bands, nall), f32),
+            dma((3, groups)), dma((3, 3)), dma((2,)), dma((groups,)), dma((groups,)),
+            dma((count,)), dma((count,)), dma((nband,)), dma((nband,)),
+            dma((nband,)), dma((count,)), dma((groups,)), dma((groups,)),
         ],
         compiler_params=pltpu.CompilerParams(
             vmem_limit_bytes=56 * 1024 * 1024, collective_id=0, has_side_effects=True
         ),
         cost_estimate=pl.CostEstimate(flops=10**11, bytes_accessed=10**7, transcendentals=0),
         name="solve",
-    )(own, *[jnp.asarray(c) for c in consts])
-
-
-def margin_kernel(count, size, orb_ref, vec_ref, o_ref, ro, rv, xo, xv, gs, gr, ps, pr,
-                  so, sv, qo, qv, sg, qg, sp, qp):
-    bands, ncell = orb_ref.shape[0], orb_ref.shape[1] * lax.axis_size("grid")
-    me, band, nband = lax.axis_index("grid"), lax.axis_index("band"), lax.axis_size("band")
-    chip, core = me // 2, me % 2
-    sib = chip * 2 + (1 - core)
-    cross = (1 - chip) * 2 + core
-    far = (1 - chip) * 2 + (1 - core)
-    mesh_id = pl.DeviceIdType.MESH
-
-    def remote(src, dst, send, recv_sem, device):
-        return pltpu.make_async_remote_copy(
-            src_ref=src, dst_ref=dst, send_sem=send, recv_sem=recv_sem,
-            device_id=device, device_id_type=mesh_id,
-        )
-
-    def each(n, body):
-        def step(k, _):
-            body(k)
-            return 0
-
-        lax.fori_loop(0, n, step, 0)
-
-    barrier = pltpu.get_barrier_semaphore()
-    each(nband, lambda b: pl.semaphore_signal(barrier, inc=1, device_id=(b, cross), device_id_type=mesh_id))
-    for other in (sib, far):
-        pl.semaphore_signal(barrier, inc=1, device_id=(band, other), device_id_type=mesh_id)
-    pl.semaphore_wait(barrier, nband + 2)
-
-    def part(src, dst, send, recv_sem, c):
-        cells = pl.ds(pl.multiple_of(c * size, 128), size)
-        return remote(src.at[:, cells], dst.at[band], send.at[c], recv_sem.at[band], (c, cross))
-
-    def target(k):
-        return (band + k) % count
-
-    each(count, lambda k: part(orb_ref, ro, so, qo, target(k)).start())
-    each(count, lambda k: part(vec_ref, rv, sv, qv, target(k)).start())
-
-    def term(b):
-        return remote(gs.at[b], gr.at[band], sg.at[b], qg.at[band], (b, cross))
-
-    @pl.when(band < count)
-    def _():
-        def take(src, dst, x, send, recv_sem):
-            def body(b):
-                cells = pl.ds(0, size)
-                remote(src.at[:, cells], dst.at[b], send.at[0], recv_sem.at[b], (b, cross)).wait_recv()
-
-            each(nband, body)
-
-            def rows(k):
-                for h in range(2):
-                    x[k, 4 * h : 4 * h + 4, :] = dst[2 * k + h]
-
-            each(nband // 2, rows)
-            return split(x[...].reshape(nband * bands, size))
-
-        oh, ol = take(orb_ref, ro, xo, so, qo)
-        vh, vl = take(vec_ref, rv, xv, sv, qv)
-
-        def nt(a, b):
-            return lax.dot_general(a, b, (((1,), (1,)), ((), ())), preferred_element_type=jnp.float32)
-
-        g = nt(vh, oh) + nt(vh, ol) + nt(vl, oh)
-        for b in range(nband):
-            gs[b] = g[4 * b : 4 * b + 4]
-        each(nband, lambda k: term((band + k) % nband).start())
-
-    def gather(c):
-        remote(gs.at[0], gr.at[c], sg.at[0], qg.at[c], (c, cross)).wait_recv()
-
-    each(count, gather)
-    total = gr[0]
-    for c in range(1, count):
-        total += gr[c]
-    ps[...] = total
-
-    def swap(slot):
-        return remote(ps, pr.at[me], sp.at[slot], qp.at[me], (band, slot))
-
-    for slot in (cross, far, sib):
-        swap(slot).start()
-    for slot in (cross, far, sib):
-        remote(ps, pr.at[slot], sp.at[slot], qp.at[slot], (band, slot)).wait()
-    pr[me] = total
-    full = (pr[0] + pr[1]) + (pr[2] + pr[3])
-    for k in range(4):
-        @pl.when(me == k)
-        def _():
-            width = o_ref.shape[1]
-            o_ref[...] = full[:, k * width : (k + 1) * width] * (1.0 / ncell)
-
-    each(count, lambda k: part(orb_ref, ro, so, qo, k).wait_send())
-    each(count, lambda k: part(vec_ref, rv, sv, qv, k).wait_send())
-
-    @pl.when(band < count)
-    def _():
-        each(nband, lambda k: term(k).wait_send())
+    )(orb, *[jnp.asarray(c) for c in consts])
 
 
 def chunking(local, nband):
     tiles = local // 128
     per = next(p for p in range(1, tiles + 1) if tiles % p == 0 and tiles // p <= nband)
     return tiles // per, per * 128
-
-
-def margin_of(orbitals, vectors):
-    bands, local = orbitals.shape
-    nband, groups = lax.axis_size("band"), lax.axis_size("grid")
-    count, size = chunking(local, nband)
-    f32, dma = jnp.float32, pltpu.SemaphoreType.DMA
-    out = pl.pallas_call(
-        functools.partial(margin_kernel, count, size),
-        out_shape=jax.ShapeDtypeStruct((bands, nband * bands // groups), f32),
-        in_specs=[pl.BlockSpec(memory_space=pltpu.VMEM)] * 2,
-        out_specs=pl.BlockSpec(memory_space=pltpu.VMEM),
-        scratch_shapes=[
-            pltpu.VMEM((nband, bands, size), f32), pltpu.VMEM((nband, bands, size), f32),
-            pltpu.VMEM((nband // 2, 8, size), f32), pltpu.VMEM((nband // 2, 8, size), f32),
-            pltpu.VMEM((nband, bands, nband * bands), f32), pltpu.VMEM((count, bands, nband * bands), f32),
-            pltpu.VMEM((bands, nband * bands), f32), pltpu.VMEM((groups, bands, nband * bands), f32),
-            dma((count,)), dma((count,)), dma((nband,)), dma((nband,)),
-            dma((nband,)), dma((count,)), dma((groups,)), dma((groups,)),
-        ],
-        compiler_params=pltpu.CompilerParams(
-            vmem_limit_bytes=24 * 1024 * 1024, collective_id=1, has_side_effects=True
-        ),
-        cost_estimate=pl.CostEstimate(flops=10**9, bytes_accessed=10**6, transcendentals=0),
-        name="margin",
-    )(orbitals, vectors)
-    return out.T
 
 
 def on_device(orbitals):
@@ -474,12 +445,10 @@
     bands, local = orbitals.shape
     ncell = local * groups
     ng = round(ncell ** (1 / 3))
-    xs, wide = local // (ng * ng), ng * ng // PTS
-    t = orbitals.reshape(bands, xs, PTS, wide // 128, 128).transpose(2, 1, 0, 3, 4)
-    out = solve(t.reshape(PTS, xs * bands, wide), bands, groups, ng)
+    raw = orbitals.reshape(bands, local // 128, 128).transpose(1, 0, 2).reshape(bands * local // 128, 128)
+    out, margin = solve(raw, bands, groups, lax.axis_size("band"), ng)
     vectors = out.reshape(local // 128, bands, 128).transpose(1, 0, 2).reshape(bands, local)
-    margin = margin_of(orbitals, vectors)
-    return (vectors, margin)
+    return (vectors, margin.T)
 
 
 def solution(mesh):

time: 92.3 us -> 82 us (0.89)
  Pallas kernels: 86.2 us -> 78.9 us
  local copies, waits for them, and re-layouts: 5.14 us -> 2.39 us
    pallas_call x2 -> x1, Pallas kernels: 86.2 us -> 78.9 us  [solve(): pl.pallas_call(functools.partial(solve_kernel, ng, count), out_shape=[jax...]
    reshape x3 -> x0, local copies, waits for them, and re-layouts: 3.45 us -> none  [the longest x1 1.41 us: on_device(): orbitals.reshape(bands, xs, PTS, wide // 128, 128).transpose(2, 1, 0, 3, 4)]
    unnamed x6 -> x4, local copies, waits for them, and re-layouts: 1.58 us -> 2.39 us
where the time goes in v3:
time: 82 us; the launch traced here: 81.9 us
  Pallas kernels  78.9 us (96%)
  local copies, waits for them, and re-layouts  2.39 us (3%)
    pallas_call x1, Pallas kernels, solve(): pl.pallas_call(functools.partial(solve_kernel, ng, count), out_shape=[jax...  78.9 us
    unnamed x4, local copies, waits for them, and re-layouts  2.39 us

profile of v3, /device:TPU:1, one launch (start us, length us, event | category | flops | bytes accessed | tf_op | source)
XLA Modules:
  0.0 81.9 jit_solution(10022969509970287063)
XLA Ops:
  0.6 78.9 %solve.1 = (f32[864,128]{1,0:T(8,128)}, f32[4,32]{1,0:T(4,128)}) custom-call(f32[864,128]{1,0:T(8,128)} %bitcast.13, f32[48,2304]{1,0:T(8,128)} %constant.10.clone.kt_ref, f32[48,768]{1,0:T(8,128)} %constant.11.clone.hz_ref, f32[2,48,768]{2,1,0:T(8,128)} %constant.12.clone.mix_ref, bf16[192,192]{1,0:T(8,128)(2,1)} %constant.13.clone.xh_ref, ...), custom_call_target="tpu_custom_call" | custom-call | flops 99999997952 | bytes 10000000 | tf_op jit(solution)/shard_map/solve/pallas_call | solution.py:407
  79.5 0.0 copy-start
  79.5 1.8 %copy.12 = f32[4,27648]{1,0:T(4,128)} copy(f32[4,27648]{1,0:T(4,128)} %bitcast.11) | data formatting | bytes 884736
  81.3 0.0 copy-done
  81.3 0.6 copy.13
Async XLA Ops:
  79.5 1.8 %copy-start = (f32[4,32]{1,0:T(4,128)S(1)}, f32[4,32]{1,0:T(4,128)}, u32[]{:S(2)}) copy-start(f32[4,32]{1,0:T(4,128)} %get-tuple-element.5) | copy-start | bytes 1540

commit v4 on v3

--- a/solution.py
+++ b/solution.py
@@ -79,8 +79,8 @@
 
 def solve_kernel(ng, count, orb_ref, kt_ref, hz_ref, mix_ref, xh_ref, xl_ref, o_ref, m_ref,
                  buf, amp, acc, ch, cl, zh, zl, cb, wh, wl, kx, vec, recv,
-                 ro, rv, xo, xv, gs, gr, ps, pr,
-                 rsem, ssem, nsem, osem, orsem, so, sv, qo, qv, sg, qg, sp, qp):
+                 ox, ro, rv, xo, xv, gs, gr, ps, pr,
+                 rsem, ssem, nsem, fsem, osem, orsem, so, sv, qo, qv, sg, qg, sp, qp):
     pts, rows, width = buf.shape[2:]
     bands, step = 4, ng // PTS
     xs = rows // bands
@@ -94,6 +94,8 @@
     above, below = (band + 1) % nband, (band + nband - 1) % nband
     mesh_id = pl.DeviceIdType.MESH
     root = np.float32(np.sqrt(0.75))
+    cuts = 3
+    per = pts // cuts
 
     def remote(src, dst, send, recv_sem, device):
         return pltpu.make_async_remote_copy(
@@ -101,8 +103,19 @@
             device_id=device, device_id_type=mesh_id,
         )
 
-    def share(blk, lane, slot, src, target):
-        return remote(src, buf.at[blk, slot], ssem.at[blk, lane], rsem.at[blk, slot], (band, target))
+    def share(blk, lane, slot, p, target):
+        piece = buf.at[blk, slot, pl.ds(per * p, per)]
+        return remote(piece, piece, ssem.at[blk, lane, p], rsem.at[blk, slot, p], (band, target))
+
+    def near(blk, p):
+        at = pl.ds(per * p, per)
+        device = (above if blk == 1 else below, cross)
+        return remote(buf.at[0, me, at], buf.at[blk, me, at], nsem.at[blk - 1, p], rsem.at[blk, me, p], device)
+
+    def onward(blk, p):
+        at = pl.ds(per * p, per)
+        device = (above if blk == 1 else below, cross)
+        return remote(buf.at[0, cross, at], buf.at[blk, cross, at], fsem.at[blk - 1], rsem.at[blk, cross, p], device)
 
     def each(n, body):
         def one(k, _):
@@ -110,8 +123,6 @@
             return 0
 
         lax.fori_loop(0, n, one, 0)
-
-    own_ref = buf.at[0, me]
 
     def lay_own(q):
         for h in range(2):
@@ -125,16 +136,76 @@
     for q in range(xs // 2):
         lay_own(q)
 
+    lanes = width // 128
+    tile, nall = 8, nband * bands
+
+    def tile_of(c):
+        return pl.ds(pl.multiple_of(c // lanes * tile, tile), tile), pl.ds(pl.multiple_of(c % lanes * 128, 128), 128)
+
+    def part_orb(c):
+        row, lane = tile_of(c)
+        mine = ro.at[pl.ds(band * bands, bands)]
+        return remote(ox.at[:, row, lane], mine, so.at[c], qo.at[band], (c, cross))
+
+    def part_vec(slot, c):
+        row, lane = tile_of(c)
+        return remote(vec.at[slot, row, lane], rv.at[band * bands + me], sv.at[slot], qv, (c, (slot + 2) % 4))
+
+    def send_vec(slot):
+        def one(k):
+            c = target(k)
+            own = jnp.logical_and(c == band, (slot + 2) % 4 == me)
+
+            @pl.when(jnp.logical_not(own))
+            def _():
+                part_vec(slot, c).start()
+
+            @pl.when(own)
+            def _():
+                row, lane = tile_of(c)
+                rv[band * bands + me] = vec[slot, row, lane]
+
+        each(count, one)
+
+    def lay_orb():
+        for r in range(pts):
+            for j in range(lanes):
+                for b in range(bands):
+                    first = bands * (lanes * r + j) + b
+                    rows_b = orb_ref[pl.ds(first, xs, stride=pts * lanes * bands), :]
+                    ox[b, xs * r : xs * r + xs, 128 * j : 128 * j + 128] = rows_b
+
+    def target(k):
+        return (band + k) % count
+
+    def term(b):
+        return remote(gs.at[b], gr.at[band], sg.at[b], qg.at[band], (b, cross))
+
+    def take(src):
+        flat = src.reshape(nall * tile, 128)
+        return split(jnp.concatenate([flat[pl.ds(r, nall, stride=tile), :] for r in range(tile)], axis=1))
+
+    def nt(a, b):
+        return lax.dot_general(a, b, (((1,), (1,)), ((), ())), preferred_element_type=jnp.float32)
+
+    def swap(slot):
+        return remote(ps, pr.at[me], sp.at[slot], qp.at[me], (band, slot))
+
+    def tiles(n, sem):
+        return remote(rv.at[pl.ds(0, n)], rv.at[pl.ds(0, n)], sem, qv, (band, sib))
+
     barrier = pltpu.get_barrier_semaphore()
     each(nband, lambda b: pl.semaphore_signal(barrier, inc=1, device_id=(b, cross), device_id_type=mesh_id))
     for other in (sib, far):
         pl.semaphore_signal(barrier, inc=1, device_id=(band, other), device_id_type=mesh_id)
     pl.semaphore_wait(barrier, nband + 2)
 
-    share(0, 1, me, own_ref, cross).start()
-    share(0, 0, me, own_ref, sib).start()
-    remote(own_ref, buf.at[1, me], nsem.at[0], rsem.at[1, me], (above, cross)).start()
-    remote(own_ref, buf.at[2, me], nsem.at[1], rsem.at[2, me], (below, cross)).start()
+    for p in range(cuts):
+        share(0, 1, me, p, cross).start()
+    for p in range(cuts):
+        share(0, 0, me, p, sib).start()
+    for p in range(cuts):
+        near(1, p).start()
 
     def weights(first, last, cols):
         def one(u, _):
@@ -157,18 +228,20 @@
         kx[pl.ds(pl.multiple_of(8 * t, 8), 8), :] = jnp.where(upper, a, b)
 
     each(ng // 2, spread_rows)
-
-    def arrived(blk, slot):
-        share(blk, 0, slot, own_ref, sib).wait_recv()
-
-    def relay(blk, slot):
-        arrived(blk, slot)
-        share(blk, 2, slot, buf.at[blk, slot], sib).start()
-
-    def spread(blk):
-        arrived(blk, cross)
-        share(blk, 1, cross, buf.at[blk, cross], cross).start()
-        share(blk, 0, cross, buf.at[blk, cross], sib).start()
+    lay_orb()
+
+    def arrived(blk, slot, p):
+        share(blk, 0, slot, p, sib).wait_recv()
+
+    def relay(blk, slot, p):
+        arrived(blk, slot, p)
+        share(blk, 2, slot, p, sib).start()
+
+    def spread(blk, p, wide):
+        arrived(blk, cross, p)
+        if wide:
+            share(blk, 1, cross, p, cross).start()
+        share(blk, 0, cross, p, sib).start()
 
     def slot_of(blk, s):
         turn = s // 2 + jnp.minimum(blk, 1)
@@ -196,21 +269,24 @@
 
         @pl.when(jnp.logical_and(blk == 0, s == 2))
         def _():
-            relay(0, cross)
-            spread(1)
+            for p in range(cuts):
+                relay(0, cross, p)
+                if p == 0:
+                    onward(1, 0).start()
+                    for k in range(cuts):
+                        near(2, k).start()
+                if p == cuts - 1:
+                    onward(2, p).start()
+                spread(1, p, p > 0)
 
         @pl.when(jnp.logical_and(blk == 1, s == 2))
         def _():
-            relay(1, me)
-            spread(2)
-
-        @pl.when(jnp.logical_and(blk == 2, s == 2))
-        def _():
-            relay(2, me)
+            spread(2, 1, True)
 
         @pl.when(s % 2 == 1)
         def _():
-            arrived(blk, slot)
+            for p in range(cuts):
+                arrived(blk, slot, p)
 
         @pl.when(blk == 0)
         def _():
@@ -278,55 +354,22 @@
                 t = [acc[slot, j, pl.ds(b, pts * xs, stride=bands), :] for b in range(bands)]
                 vec[slot, :, 128 * j : 128 * j + 128] = -((t[0] + t[1]) + (t[2] + t[3]))
 
-            @pl.when(s < 3)
-            def _():
-                push(slot).start()
-
-    size = orb_ref.shape[0] // count
-
-    def part(src, dst, send, recv_sem, c):
-        cells = pl.ds(pl.multiple_of(c * size, 8), size)
-        return remote(src.at[cells], dst.at[band], send.at[c], recv_sem.at[band], (c, cross))
-
-    def target(k):
-        return (band + k) % count
-
-    def term(b):
-        return remote(gs.at[b], gr.at[band], sg.at[b], qg.at[band], (b, cross))
-
-    def take(src, dst, x, send, recv_sem):
-        def body(b):
-            remote(src.at[pl.ds(0, size)], dst.at[b], send.at[0], recv_sem.at[b], (b, cross)).wait_recv()
-
-        each(nband, body)
-
-        def lay(k):
-            for h in range(2):
-                for t in range(size // bands):
-                    row = dst[2 * k + h, bands * t : bands * t + bands, :]
-                    x[k, 4 * h : 4 * h + 4, 128 * t : 128 * t + 128] = row
-
-        each(nband // 2, lay)
-
-    def nt(a, b):
-        return lax.dot_general(a, b, (((1,), (1,)), ((), ())), preferred_element_type=jnp.float32)
-
-    def swap(slot):
-        return remote(ps, pr.at[me], sp.at[slot], qp.at[me], (band, slot))
+            send_vec(slot)
 
     def margin():
-        wide = size // bands * 128
-
         @pl.when(band < count)
         def _():
-            take(orb_ref, ro, xo, so, qo)
-            oh, ol = split(xo[...].reshape(nband * bands, wide))
-            take(o_ref, rv, xv, sv, qv)
-            vh, vl = split(xv[...].reshape(nband * bands, wide))
-            g = nt(vh, oh) + nt(vh, ol) + nt(vl, oh)
+            each(nband, lambda b: remote(ox.at[:, pl.ds(0, tile), pl.ds(0, 128)], ro.at[pl.ds(b * bands, bands)],
+                                         so.at[0], qo.at[b], (b, cross)).wait_recv())
+            xo[...], xv[...] = take(ro)
+            tiles(nall - 1, sv.at[0]).wait_recv()
+            vh, vl = take(rv)
+            g = nt(vh, xo[...]) + nt(vh, xv[...]) + nt(vl, xo[...])
             for b in range(nband):
                 gs[b] = g[4 * b : 4 * b + 4]
             each(nband, lambda k: term((band + k) % nband).start())
+
+        collect()
 
         def gather(c):
             remote(gs.at[0], gr.at[c], sg.at[0], qg.at[c], (c, cross)).wait_recv()
@@ -350,13 +393,26 @@
     def block(blk):
         each(4, lambda s: forward(blk, s))
         planar(0, ch, cl, keep_split)
+
+        @pl.when(blk == 1)
+        def _():
+            spread(2, 2, False)
+
         xconv()
+        planar(1, zh, zl, keep)
+
+        @pl.when(blk == 0)
+        def _():
+            spread(2, 0, True)
+            for p in range(cuts):
+                relay(1, me, p)
 
         @pl.when(blk == 1)
         def _():
-            each(count, lambda k: part(orb_ref, ro, so, qo, target(k)).start())
-
-        planar(1, zh, zl, keep)
+            for p in range(cuts):
+                relay(2, me, p)
+            each(count, lambda k: part_orb(target(k)).start())
+
         each(4, lambda s: inverse(blk, s))
 
     each(3, block)
@@ -367,25 +423,39 @@
                 piece = src[xs * r : xs * r + xs, 128 * j : 128 * j + 128]
                 o_ref[pl.ds(bands * (width // 128 * r + j) + slot, xs, stride=pts * width // 128 * bands), :] = piece
 
-    recv[me] = vec[me]
-    for slot in (sib, cross, far):
-        remote(vec.at[slot], recv.at[slot], osem.at[slot], orsem.at[slot], (band, slot)).wait()
-    for k in range(4):
-        place(k, recv[k])
-    each(count, lambda k: part(o_ref, rv, sv, qv, target(k)).start())
+    for slot in (cross, far, sib):
+        push(slot).start()
+
+    def collect():
+        recv[me] = vec[me]
+        for slot in (sib, cross, far):
+            remote(vec.at[slot], recv.at[slot], osem.at[slot], orsem.at[slot], (band, slot)).wait()
+        for k in range(4):
+            place(k, recv[k])
+
     margin()
-    each(count, lambda k: part(orb_ref, ro, so, qo, k).wait_send())
-    each(count, lambda k: part(o_ref, rv, sv, qv, k).wait_send())
+    each(count, lambda k: part_orb(k).wait_send())
+    for slot in range(4):
+        tiles(count - 1, sv.at[slot]).wait_send()
+
+        @pl.when(jnp.logical_or(band >= count, (slot + 2) % 4 != me))
+        def _():
+            tiles(1, sv.at[slot]).wait_send()
 
     @pl.when(band < count)
     def _():
         each(nband, lambda k: term(k).wait_send())
 
-    for blk in range(3):
-        for lane, target in ((0, sib), (1, cross), (2, sib)):
-            share(blk, lane, me, own_ref, target).wait_send()
-    remote(own_ref, buf.at[1, me], nsem.at[0], rsem.at[1, me], (above, cross)).wait_send()
-    remote(own_ref, buf.at[2, me], nsem.at[1], rsem.at[2, me], (below, cross)).wait_send()
+    for p in range(cuts):
+        for blk in range(3):
+            share(blk, 0, me, p, sib).wait_send()
+            share(blk, 2, me, p, sib).wait_send()
+            if (blk, p) not in ((1, 0), (2, cuts - 1)):
+                share(blk, 1, me, p, cross).wait_send()
+        near(1, p).wait_send()
+        near(2, p).wait_send()
+    onward(1, 0).wait_send()
+    onward(2, cuts - 1).wait_send()
 
 
 def solve(orb, bands, groups, nband, ng):
@@ -401,8 +471,7 @@
     f32, bf16, dma = jnp.float32, jnp.bfloat16, pltpu.SemaphoreType.DMA
     tall = groups * rows
     xs = rows // bands
-    count, wide = chunking(orb.shape[0] * 128 // bands, nband)
-    size, nall = wide * bands // 128, nband * bands
+    count, nall = orb.shape[0] // bands // 8, nband * bands
     vmem = pl.BlockSpec(memory_space=pltpu.VMEM)
     return pl.pallas_call(
         functools.partial(solve_kernel, ng, count),
@@ -418,12 +487,59 @@
             pltpu.VMEM((2, total, 2 * width), bf16), pltpu.VMEM((2, total, 2 * width), bf16),
             pltpu.VMEM((tall, total), f32),
             pltpu.VMEM((groups, pts * xs, width), f32), pltpu.VMEM((groups, pts * xs, width), f32),
-            pltpu.VMEM((nband, size, 128), f32), pltpu.VMEM((nband, size, 128), f32),
-            pltpu.VMEM((nband // 2, 8, wide), f32), pltpu.VMEM((nband // 2, 8, wide), f32),
+            pltpu.VMEM((bands, pts * xs, width), f32),
+            pltpu.VMEM((nall, 8, 128), f32), pltpu.VMEM((nall, 8, 128), f32),
+            pltpu.VMEM((nall, 1024), bf16), pltpu.VMEM((nall, 1024), bf16),
             pltpu.VMEM((nband, bands, nall), f32), pltpu.VMEM((count, bands, nall), f32),
             pltpu.VMEM((bands, nall), f32), pltpu.VMEM((groups, bands, nall), f32),
-            dma((3, groups)), dma((3, 3)), dma((2,)), dma((groups,)), dma((groups,)),
-            dma((count,)), dma((count,)), dma((nband,)), dma((nband,)),
+            dma((3, groups, 3)), dma((3, 3, 3)), dma((2, 3)), dma((2,)), dma((groups,)), dma((groups,)),
+            dma((count,)), dma((groups,)), dma((nband,)), dma(()),
+            dma((nband,)), dma((count,)), dma((groups,)), dma((groups,)),
+        ],
+        compiler_params=pltpu.CompilerParams(
+            vmem_limit_bytes=56 * 1024 * 1024, collective_id=0, has_side_effects=True
+        ),
+        cost_estimate=pl.CostEstimate(flops=10**11, bytes_accessed=10**7, transcendentals=0),
+        name="solve",
+    )(orb, *[jnp.asarray(c) for c in consts])
+
+
+def solve(orb, bands, groups, nband, ng):
+    width = ng * ng // PTS
+    pts, rows = PTS, orb.shape[0] * 128 // (PTS * width)
+    step = ng // PTS
+    total = pts * width
+    xh, xl = split_const(np.kron(hartley(ng), np.eye(bands)))
+    hz = np.tile(hartley(ng), (1, 2 * step)).astype(np.float32)
+    kt = (kernel_values(ng).astype(np.float32) / np.float32(ng**3)).reshape(ng, total)
+    consts = [kt, hz, mixer_rows(ng).astype(np.float32), xh, xl]
+    full = (groups, pts, rows, width)
+    f32, bf16, dma = jnp.float32, jnp.bfloat16, pltpu.SemaphoreType.DMA
+    tall = groups * rows
+    xs = rows // bands
+    count, nall = orb.shape[0] // bands // 8, nband * bands
+    vmem = pl.BlockSpec(memory_space=pltpu.VMEM)
+    return pl.pallas_call(
+        functools.partial(solve_kernel, ng, count),
+        out_shape=[jax.ShapeDtypeStruct(orb.shape, f32), jax.ShapeDtypeStruct((bands, nall // groups), f32)],
+        in_specs=[vmem] * 6,
+        out_specs=[vmem] * 2,
+        scratch_shapes=[
+            pltpu.VMEM((3,) + full, f32), pltpu.VMEM(full, f32),
+            pltpu.VMEM((groups, width // 128, pts * rows, 128), f32),
+            pltpu.VMEM((tall, total), bf16), pltpu.VMEM((tall, total), bf16),
+            pltpu.VMEM((tall, total), bf16), pltpu.VMEM((tall, total), bf16),
+            pltpu.VMEM((tall, total), f32),
+            pltpu.VMEM((2, total, 2 * width), bf16), pltpu.VMEM((2, total, 2 * width), bf16),
+            pltpu.VMEM((tall, total), f32),
+            pltpu.VMEM((groups, pts * xs, width), f32), pltpu.VMEM((groups, pts * xs, width), f32),
+            pltpu.VMEM((bands, pts * xs, width), f32),
+            pltpu.VMEM((nall, 8, 128), f32), pltpu.VMEM((nall, 8, 128), f32),
+            pltpu.VMEM((nall, 1024), bf16), pltpu.VMEM((nall, 1024), bf16),
+            pltpu.VMEM((nband, bands, nall), f32), pltpu.VMEM((count, bands, nall), f32),
+            pltpu.VMEM((bands, nall), f32), pltpu.VMEM((groups, bands, nall), f32),
+            dma((3, groups, 3)), dma((3, 3, 3)), dma((2, 3)), dma((2,)), dma((groups,)), dma((groups,)),
+            dma((count,)), dma((groups,)), dma((nband,)), dma(()),
             dma((nband,)), dma((count,)), dma((groups,)), dma((groups,)),
         ],
         compiler_params=pltpu.CompilerParams(

time: 82 us -> 73.4 us (0.90)
  Pallas kernels: 78.9 us -> 70.2 us
    pallas_call x1, Pallas kernels: 78.9 us -> 70.2 us  [solve(): pl.pallas_call(functools.partial(solve_kernel, ng, count), out_shape=[jax...]
where the time goes in v4:
time: 73.4 us; the launch traced here: 73.3 us
  Pallas kernels  70.2 us (96%)
  local copies, waits for them, and re-layouts  2.39 us (3%)
    pallas_call x1, Pallas kernels, solve(): pl.pallas_call(functools.partial(solve_kernel, ng, count), out_shape=[jax...  70.2 us
    unnamed x4, local copies, waits for them, and re-layouts  2.39 us

profile of v4, /device:TPU:1, one launch (start us, length us, event | category | flops | bytes accessed | tf_op | source)
XLA Modules:
  0.0 73.3 jit_solution(5280375555579243428)
XLA Ops:
  0.6 70.2 %solve.1 = (f32[864,128]{1,0:T(8,128)}, f32[4,32]{1,0:T(4,128)}) custom-call(f32[864,128]{1,0:T(8,128)} %bitcast.13, f32[48,2304]{1,0:T(8,128)} %constant.10.clone.kt_ref, f32[48,768]{1,0:T(8,128)} %constant.11.clone.hz_ref, f32[2,48,768]{2,1,0:T(8,128)} %constant.12.clone.mix_ref, bf16[192,192]{1,0:T(8,128)(2,1)} %constant.13.clone.xh_ref, ...), custom_call_target="tpu_custom_call" | custom-call | flops 99999997952 | bytes 10000000 | tf_op jit(solution)/shard_map/solve/pallas_call | solution.py:522
  70.9 0.0 copy-start
  70.9 1.8 %copy.12 = f32[4,27648]{1,0:T(4,128)} copy(f32[4,27648]{1,0:T(4,128)} %bitcast.11) | data formatting | bytes 884736
  72.7 0.0 copy-done
  72.7 0.6 copy.13
Async XLA Ops:
  70.9 1.8 %copy-start = (f32[4,32]{1,0:T(4,128)S(1)}, f32[4,32]{1,0:T(4,128)}, u32[]{:S(2)}) copy-start(f32[4,32]{1,0:T(4,128)} %get-tuple-element.5) | copy-start | bytes 1540

commit v5 on v4

--- a/solution.py
+++ b/solution.py
@@ -79,8 +79,8 @@
 
 def solve_kernel(ng, count, orb_ref, kt_ref, hz_ref, mix_ref, xh_ref, xl_ref, o_ref, m_ref,
                  buf, amp, acc, ch, cl, zh, zl, cb, wh, wl, kx, vec, recv,
-                 ox, ro, rv, xo, xv, gs, gr, ps, pr,
-                 rsem, ssem, nsem, fsem, osem, orsem, so, sv, qo, qv, sg, qg, sp, qp):
+                 ox, ro, rv, xo, xv, gs, gr,
+                 rsem, ssem, nsem, fsem, osem, orsem, so, sv, qo, qv, sg, qg):
     pts, rows, width = buf.shape[2:]
     bands, step = 4, ng // PTS
     xs = rows // bands
@@ -139,33 +139,55 @@
     lanes = width // 128
     tile, nall = 8, nband * bands
 
-    def tile_of(c):
-        return pl.ds(pl.multiple_of(c // lanes * tile, tile), tile), pl.ds(pl.multiple_of(c % lanes * 128, 128), 128)
-
-    def part_orb(c):
-        row, lane = tile_of(c)
+    deep = pts * xs // tile
+    own_row, own_lane = band // lanes, band % lanes
+    first_row, first_band = (own_row + deep * 5 // 8) % deep, (band + nband * 5 // 8) % nband
+
+    def wrap(n, top):
+        return jnp.where(n >= top, n - top, n)
+
+    def cells(row, j):
+        return pl.ds(pl.multiple_of(row * tile, tile), tile), pl.ds(128 * j, 128)
+
+    def part_orb(row, j):
         mine = ro.at[pl.ds(band * bands, bands)]
-        return remote(ox.at[:, row, lane], mine, so.at[c], qo.at[band], (c, cross))
-
-    def part_vec(slot, c):
-        row, lane = tile_of(c)
-        return remote(vec.at[slot, row, lane], rv.at[band * bands + me], sv.at[slot], qv, (c, (slot + 2) % 4))
+        r, l = cells(row, j)
+        return remote(ox.at[:, r, l], mine, so, qo, (row * lanes + j, cross))
+
+    def send_orb():
+        def one(k):
+            for j in range(lanes):
+                part_orb(wrap(first_row + k, deep), j).start()
+
+        each(deep, one)
+
+    def part_vec(slot, row, j):
+        r, l = cells(row, j)
+        return remote(vec.at[slot, r, l], rv.at[band * bands + me], sv.at[slot], qv, (row * lanes + j, (slot + 2) % 4))
 
     def send_vec(slot):
         def one(k):
-            c = target(k)
-            own = jnp.logical_and(c == band, (slot + 2) % 4 == me)
-
-            @pl.when(jnp.logical_not(own))
+            row = wrap(first_row + k, deep)
+            home = jnp.logical_and(row == own_row, (slot + 2) % 4 == me)
+
+            @pl.when(jnp.logical_not(home))
             def _():
-                part_vec(slot, c).start()
-
-            @pl.when(own)
+                for j in range(lanes):
+                    part_vec(slot, row, j).start()
+
+            @pl.when(home)
             def _():
-                row, lane = tile_of(c)
-                rv[band * bands + me] = vec[slot, row, lane]
-
-        each(count, one)
+                for j in range(lanes):
+                    @pl.when(own_lane != j)
+                    def _():
+                        part_vec(slot, row, j).start()
+
+                    @pl.when(own_lane == j)
+                    def _():
+                        r, l = cells(row, j)
+                        rv[band * bands + me] = vec[slot, r, l]
+
+        each(deep, one)
 
     def lay_orb():
         for r in range(pts):
@@ -175,11 +197,44 @@
                     rows_b = orb_ref[pl.ds(first, xs, stride=pts * lanes * bands), :]
                     ox[b, xs * r : xs * r + xs, 128 * j : 128 * j + 128] = rows_b
 
-    def target(k):
-        return (band + k) % count
-
-    def term(b):
-        return remote(gs.at[b], gr.at[band], sg.at[b], qg.at[band], (b, cross))
+    def term(b, g):
+        return remote(gs.at[b * bands + g], gr.at[band * bands + me], sg, qg, (b, g))
+
+    def terms(n):
+        return remote(gs.at[pl.ds(0, n)], gs.at[pl.ds(0, n)], sg, qg, (band, sib))
+
+    def send_terms():
+        def one(k):
+            b = wrap(first_band + k, nband)
+
+            @pl.when(b != band)
+            def _():
+                for g in range(bands):
+                    term(b, g).start()
+
+            @pl.when(b == band)
+            def _():
+                for g in range(bands):
+                    @pl.when(me != g)
+                    def _():
+                        term(b, g).start()
+
+                    @pl.when(me == g)
+                    def _():
+                        gr[band * bands + me] = gs[b * bands + g]
+
+        each(nband, one)
+
+    def regroup(g):
+        sub = lax.broadcasted_iota(jnp.int32, (nall, nall), 0) % bands
+        quarter = nall // bands
+        lane = lax.broadcasted_iota(jnp.int32, (nall, nall), 1) // quarter
+        out = g
+        for d in range(1, bands):
+            moved = jnp.where(sub >= d, pltpu.roll(g, d, 0), pltpu.roll(g, nall + d - bands, 0))
+            moved = pltpu.roll(moved, nall - quarter * d, 1)
+            out = jnp.where((sub + bands - lane) % bands == d, moved, out)
+        return out
 
     def take(src):
         flat = src.reshape(nall * tile, 128)
@@ -187,9 +242,6 @@
 
     def nt(a, b):
         return lax.dot_general(a, b, (((1,), (1,)), ((), ())), preferred_element_type=jnp.float32)
-
-    def swap(slot):
-        return remote(ps, pr.at[me], sp.at[slot], qp.at[me], (band, slot))
 
     def tiles(n, sem):
         return remote(rv.at[pl.ds(0, n)], rv.at[pl.ds(0, n)], sem, qv, (band, sib))
@@ -307,20 +359,20 @@
 
     groups = ((0, 1), (1, 1), (2, 2), (4, 2))
 
-    def planar(d, ah, al, emit):
+    def planar(d, ah, al, emit, at):
         for first, count in groups:
             lo, size = first * width, count * width
             for n in range(0, size, 256):
                 w = min(256, size - n)
-                a, b = ah[:, lo : lo + size], al[:, lo : lo + size]
+                a, b = ah[at, lo : lo + size], al[at, lo : lo + size]
                 g, h = wh[d, lo : lo + size, n : n + w], wl[d, lo : lo + size, n : n + w]
-                emit(lo + n, w, mm(a, g) + mm(b, g) + mm(a, h))
-
-    def keep_split(at, w, v):
-        zh[:, at : at + w], zl[:, at : at + w] = split(v)
-
-    def keep(at, w, v):
-        cb[:, at : at + w] = v
+                emit(at, slice(lo + n, lo + n + w), mm(a, g) + mm(b, g) + mm(a, h))
+
+    def keep_split(at, to, v):
+        zh[at, to], zl[at, to] = split(v)
+
+    def keep(at, to, v):
+        cb[at, to] = v
 
     def xpass(h, l):
         return mm(xh_ref[...], h) + mm(xh_ref[...], l) + mm(xl_ref[...], h)
@@ -359,47 +411,50 @@
     def margin():
         @pl.when(band < count)
         def _():
-            each(nband, lambda b: remote(ox.at[:, pl.ds(0, tile), pl.ds(0, 128)], ro.at[pl.ds(b * bands, bands)],
-                                         so.at[0], qo.at[b], (b, cross)).wait_recv())
+            remote(ro, ro, so, qo, (band, cross)).wait_recv()
             xo[...], xv[...] = take(ro)
             tiles(nall - 1, sv.at[0]).wait_recv()
             vh, vl = take(rv)
             g = nt(vh, xo[...]) + nt(vh, xv[...]) + nt(vl, xo[...])
-            for b in range(nband):
-                gs[b] = g[4 * b : 4 * b + 4]
-            each(nband, lambda k: term((band + k) % nband).start())
+            g = regroup(g)
+            for n in range(nall):
+                gs[n] = g[n : n + 1]
+            send_terms()
 
         collect()
-
-        def gather(c):
-            remote(gs.at[0], gr.at[c], sg.at[0], qg.at[c], (c, cross)).wait_recv()
-
-        each(count, gather)
-        sums = gr[0]
-        for c in range(1, count):
-            sums += gr[c]
-        ps[...] = sums
-        for slot in (cross, far, sib):
-            swap(slot).start()
-        for slot in (cross, far, sib):
-            remote(ps, pr.at[slot], sp.at[slot], qp.at[slot], (band, slot)).wait()
-        pr[me] = sums
-        full = ((pr[0] + pr[1]) + (pr[2] + pr[3])) * (1.0 / ng**3)
-        for k in range(4):
-            @pl.when(me == k)
-            def _():
-                m_ref[...] = full[:, k * m_ref.shape[1] : (k + 1) * m_ref.shape[1]]
+        drain()
+
+        held = count * bands
+        @pl.when(band < count)
+        def _():
+            terms(held - 1).wait_recv()
+
+        @pl.when(band >= count)
+        def _():
+            terms(held).wait_recv()
+
+        sums = [gr[n] for n in range(4)]
+        for n in range(4, held):
+            sums[n % 4] += gr[n]
+        full = ((sums[0] + sums[1]) + (sums[2] + sums[3])) * (1.0 / ng**3)
+        for k in range(bands):
+            m_ref[k : k + 1, :] = full[:, k * m_ref.shape[1] : (k + 1) * m_ref.shape[1]]
 
     def block(blk):
-        each(4, lambda s: forward(blk, s))
-        planar(0, ch, cl, keep_split)
+        def half(h):
+            forward(blk, 2 * h)
+            forward(blk, 2 * h + 1)
+            which = (chip + jnp.minimum(blk, 1) + h) % 2
+            planar(0, ch, cl, keep_split, pl.ds(pl.multiple_of(which * 2 * rows, 32), 2 * rows))
+
+        each(2, half)
 
         @pl.when(blk == 1)
         def _():
             spread(2, 2, False)
 
         xconv()
-        planar(1, zh, zl, keep)
+        planar(1, zh, zl, keep, slice(None))
 
         @pl.when(blk == 0)
         def _():
@@ -411,7 +466,7 @@
         def _():
             for p in range(cuts):
                 relay(2, me, p)
-            each(count, lambda k: part_orb(target(k)).start())
+            send_orb()
 
         each(4, lambda s: inverse(blk, s))
 
@@ -433,29 +488,35 @@
         for k in range(4):
             place(k, recv[k])
 
+    def drain():
+        remote(ox, ox, so, qo, (band, cross)).wait_send()
+        for slot in range(4):
+            home = jnp.logical_and(band < count, (slot + 2) % 4 == me)
+
+            @pl.when(home)
+            def _():
+                tiles(count - 1, sv.at[slot]).wait_send()
+
+            @pl.when(jnp.logical_not(home))
+            def _():
+                tiles(count, sv.at[slot]).wait_send()
+
+        for p in range(cuts):
+            for blk in range(3):
+                share(blk, 0, me, p, sib).wait_send()
+                share(blk, 2, me, p, sib).wait_send()
+                if (blk, p) not in ((1, 0), (2, cuts - 1)):
+                    share(blk, 1, me, p, cross).wait_send()
+            near(1, p).wait_send()
+            near(2, p).wait_send()
+        onward(1, 0).wait_send()
+        onward(2, cuts - 1).wait_send()
+
     margin()
-    each(count, lambda k: part_orb(k).wait_send())
-    for slot in range(4):
-        tiles(count - 1, sv.at[slot]).wait_send()
-
-        @pl.when(jnp.logical_or(band >= count, (slot + 2) % 4 != me))
-        def _():
-            tiles(1, sv.at[slot]).wait_send()
 
     @pl.when(band < count)
     def _():
-        each(nband, lambda k: term(k).wait_send())
-
-    for p in range(cuts):
-        for blk in range(3):
-            share(blk, 0, me, p, sib).wait_send()
-            share(blk, 2, me, p, sib).wait_send()
-            if (blk, p) not in ((1, 0), (2, cuts - 1)):
-                share(blk, 1, me, p, cross).wait_send()
-        near(1, p).wait_send()
-        near(2, p).wait_send()
-    onward(1, 0).wait_send()
-    onward(2, cuts - 1).wait_send()
+        terms(nall - 1).wait_send()
 
 
 def solve(orb, bands, groups, nband, ng):
@@ -475,7 +536,7 @@
     vmem = pl.BlockSpec(memory_space=pltpu.VMEM)
     return pl.pallas_call(
         functools.partial(solve_kernel, ng, count),
-        out_shape=[jax.ShapeDtypeStruct(orb.shape, f32), jax.ShapeDtypeStruct((bands, nall // groups), f32)],
+        out_shape=[pltpu.VMEM(orb.shape, f32), pltpu.VMEM((bands, nall // groups), f32)],
         in_specs=[vmem] * 6,
         out_specs=[vmem] * 2,
         scratch_shapes=[
@@ -490,11 +551,10 @@
             pltpu.VMEM((bands, pts * xs, width), f32),
             pltpu.VMEM((nall, 8, 128), f32), pltpu.VMEM((nall, 8, 128), f32),
             pltpu.VMEM((nall, 1024), bf16), pltpu.VMEM((nall, 1024), bf16),
-            pltpu.VMEM((nband, bands, nall), f32), pltpu.VMEM((count, bands, nall), f32),
-            pltpu.VMEM((bands, nall), f32), pltpu.VMEM((groups, bands, nall), f32),
+            pltpu.VMEM((nall, 1, nall), f32), pltpu.VMEM((count * groups, 1, nall), f32),
             dma((3, groups, 3)), dma((3, 3, 3)), dma((2, 3)), dma((2,)), dma((groups,)), dma((groups,)),
-            dma((count,)), dma((groups,)), dma((nband,)), dma(()),
-            dma((nband,)), dma((count,)), dma((groups,)), dma((groups,)),
+            dma(()), dma((groups,)), dma(()), dma(()),
+            dma(()), dma(()),
         ],
         compiler_params=pltpu.CompilerParams(
             vmem_limit_bytes=56 * 1024 * 1024, collective_id=0, has_side_effects=True
@@ -502,58 +562,6 @@
         cost_estimate=pl.CostEstimate(flops=10**11, bytes_accessed=10**7, transcendentals=0),
         name="solve",
     )(orb, *[jnp.asarray(c) for c in consts])
-
-
-def solve(orb, bands, groups, nband, ng):
-    width = ng * ng // PTS
-    pts, rows = PTS, orb.shape[0] * 128 // (PTS * width)
-    step = ng // PTS
-    total = pts * width
-    xh, xl = split_const(np.kron(hartley(ng), np.eye(bands)))
-    hz = np.tile(hartley(ng), (1, 2 * step)).astype(np.float32)
-    kt = (kernel_values(ng).astype(np.float32) / np.float32(ng**3)).reshape(ng, total)
-    consts = [kt, hz, mixer_rows(ng).astype(np.float32), xh, xl]
-    full = (groups, pts, rows, width)
-    f32, bf16, dma = jnp.float32, jnp.bfloat16, pltpu.SemaphoreType.DMA
-    tall = groups * rows
-    xs = rows // bands
-    count, nall = orb.shape[0] // bands // 8, nband * bands
-    vmem = pl.BlockSpec(memory_space=pltpu.VMEM)
-    return pl.pallas_call(
-        functools.partial(solve_kernel, ng, count),
-        out_shape=[jax.ShapeDtypeStruct(orb.shape, f32), jax.ShapeDtypeStruct((bands, nall // groups), f32)],
-        in_specs=[vmem] * 6,
-        out_specs=[vmem] * 2,
-        scratch_shapes=[
-            pltpu.VMEM((3,) + full, f32), pltpu.VMEM(full, f32),
-            pltpu.VMEM((groups, width // 128, pts * rows, 128), f32),
-            pltpu.VMEM((tall, total), bf16), pltpu.VMEM((tall, total), bf16),
-            pltpu.VMEM((tall, total), bf16), pltpu.VMEM((tall, total), bf16),
-            pltpu.VMEM((tall, total), f32),
-            pltpu.VMEM((2, total, 2 * width), bf16), pltpu.VMEM((2, total, 2 * width), bf16),
-            pltpu.VMEM((tall, total), f32),
-            pltpu.VMEM((groups, pts * xs, width), f32), pltpu.VMEM((groups, pts * xs, width), f32),
-            pltpu.VMEM((bands, pts * xs, width), f32),
-            pltpu.VMEM((nall, 8, 128), f32), pltpu.VMEM((nall, 8, 128), f32),
-            pltpu.VMEM((nall, 1024), bf16), pltpu.VMEM((nall, 1024), bf16),
-            pltpu.VMEM((nband, bands, nall), f32), pltpu.VMEM((count, bands, nall), f32),
-            pltpu.VMEM((bands, nall), f32), pltpu.VMEM((groups, bands, nall), f32),
-            dma((3, groups, 3)), dma((3, 3, 3)), dma((2, 3)), dma((2,)), dma((groups,)), dma((groups,)),
-            dma((count,)), dma((groups,)), dma((nband,)), dma(()),
-            dma((nband,)), dma((count,)), dma((groups,)), dma((groups,)),
-        ],
-        compiler_params=pltpu.CompilerParams(
-            vmem_limit_bytes=56 * 1024 * 1024, collective_id=0, has_side_effects=True
-        ),
-        cost_estimate=pl.CostEstimate(flops=10**11, bytes_accessed=10**7, transcendentals=0),
-        name="solve",
-    )(orb, *[jnp.asarray(c) for c in consts])
-
-
-def chunking(local, nband):
-    tiles = local // 128
-    per = next(p for p in range(1, tiles + 1) if tiles % p == 0 and tiles // p <= nband)
-    return tiles // per, per * 128
 
 
 def on_device(orbitals):

time: 73.4 us -> 69.1 us (0.941)
  Pallas kernels: 70.2 us -> 67 us
  local copies, waits for them, and re-layouts: 2.39 us -> 1.34 us
    pallas_call x1, Pallas kernels: 70.2 us -> 67 us  [solve(): pl.pallas_call(functools.partial(solve_kernel, ng, count), out_shape=[plt...]
    unnamed x4 -> x2, local copies, waits for them, and re-layouts: 2.39 us -> 1.34 us
where the time goes in v5:
time: 69.1 us; the launch traced here: 69 us
  Pallas kernels  67 us (97%)
  local copies, waits for them, and re-layouts  1.34 us (2%)
    pallas_call x1, Pallas kernels, solve(): pl.pallas_call(functools.partial(solve_kernel, ng, count), out_shape=[plt...  67 us

profile of v5, /device:TPU:1, one launch (start us, length us, event | category | flops | bytes accessed | tf_op | source)
XLA Modules:
  0.0 69.0 jit_solution(5381662743237465240)
XLA Ops:
  0.6 67.0 %solve.1 = (f32[864,128]{1,0:T(8,128)S(1)}, f32[4,32]{1,0:T(4,128)S(1)}) custom-call(f32[864,128]{1,0:T(8,128)} %bitcast.13, f32[48,2304]{1,0:T(8,128)} %constant.10.clone.kt_ref, f32[48,768]{1,0:T(8,128)} %constant.11.clone.hz_ref, f32[2,48,768]{2,1,0:T(8,128)} %constant.12.clone.mix_ref, bf16[192,192]{1,0:T(8,128)(2,1)} %constant.13.clone.xh_ref, ...), custom_call_target="tpu_custom_call" | custom-call | flops 99999997952 | bytes 10000000 | tf_op jit(solution)/shard_map/solve/pallas_call | solution.py:537
  67.7 0.8 %copy.12 = f32[4,27648]{1,0:T(4,128)} copy(f32[4,27648]{1,0:T(4,128)S(1)} %bitcast.11) | data formatting | bytes 884736
  68.4 0.6 copy.13

commit v6 on v5

--- a/solution.py
+++ b/solution.py
@@ -77,9 +77,9 @@
     return jnp.dot(a, b, preferred_element_type=jnp.float32)
 
 
-def solve_kernel(ng, count, orb_ref, kt_ref, hz_ref, mix_ref, xh_ref, xl_ref, o_ref, m_ref,
+def solve_kernel(ng, orb_ref, kt_ref, hz_ref, mix_ref, xh_ref, xl_ref, o_ref, m_ref,
                  buf, amp, acc, ch, cl, zh, zl, cb, wh, wl, kx, vec, recv,
-                 ox, ro, rv, xo, xv, gs, gr,
+                 ox, st, ro, rv, xo, xv, ga, gs, gr,
                  rsem, ssem, nsem, fsem, osem, orsem, so, sv, qo, qv, sg, qg):
     pts, rows, width = buf.shape[2:]
     bands, step = 4, ng // PTS
@@ -138,56 +138,86 @@
 
     lanes = width // 128
     tile, nall = 8, nband * bands
-
-    deep = pts * xs // tile
-    own_row, own_lane = band // lanes, band % lanes
-    first_row, first_band = (own_row + deep * 5 // 8) % deep, (band + nband * 5 // 8) % nband
-
-    def wrap(n, top):
-        return jnp.where(n >= top, n - top, n)
-
-    def cells(row, j):
-        return pl.ds(pl.multiple_of(row * tile, tile), tile), pl.ds(128 * j, 128)
-
-    def part_orb(row, j):
-        mine = ro.at[pl.ds(band * bands, bands)]
-        r, l = cells(row, j)
-        return remote(ox.at[:, r, l], mine, so, qo, (row * lanes + j, cross))
-
-    def send_orb():
-        def one(k):
-            for j in range(lanes):
-                part_orb(wrap(first_row + k, deep), j).start()
-
-        each(deep, one)
-
-    def part_vec(slot, row, j):
-        r, l = cells(row, j)
-        return remote(vec.at[slot, r, l], rv.at[band * bands + me], sv.at[slot], qv, (row * lanes + j, (slot + 2) % 4))
-
-    def send_vec(slot):
-        def one(k):
-            row = wrap(first_row + k, deep)
-            home = jnp.logical_and(row == own_row, (slot + 2) % 4 == me)
+    yy, zz, xh = band % 8 // 2, band // 8, band % 2
+    moves = ((0, 0), (1, 0), (3, 0), (0, 1), (0, 3), (1, 1), (1, 3), (2, 0))
+    share_of = 2 * len(moves)
+    extra = pts * xs * lanes // tile - share_of
+
+    def base(y, z):
+        return z % 4 * 8 + y % 4 * 2
+
+    def shade(y, z):
+        return (y + z // 2 * 2) % 4 + z % 2 * 4
+
+    targets = [(base(yy + oy, zz + oz), shade((yy + oy) % 4, (zz + oz) % 4)) for oy, oz in moves]
+    sources = [base(yy + 4 - oy, zz + 4 - oz) for oy, oz in moves]
+    double = shade(yy, zz) + 8 * xh < extra
+
+    def tile_at(t):
+        return pl.ds(pl.multiple_of(t * tile, tile), tile)
+
+    def send_orb(src, b):
+        mine = pl.ds(b * bands, bands)
+
+        def one(e, y, z, k):
+            home = jnp.logical_and(yy == y, zz == z)
+            at = tile_at(e + 8 * xh + share_of * k)
 
             @pl.when(jnp.logical_not(home))
             def _():
-                for j in range(lanes):
-                    part_vec(slot, row, j).start()
+                remote(src.at[:, at], ro.at[k, mine], so.at[k], qo.at[k], (base(y, z) + xh, me)).start()
 
             @pl.when(home)
             def _():
-                for j in range(lanes):
-                    @pl.when(own_lane != j)
+                ro[k, mine] = src[:, at]
+
+        for e in range(8):
+            for w in range(2):
+                y, z = (e % 4 + 2 * w) % 4, e // 4 + 2 * w
+                one(e, y, z, 0)
+                if e + 8 < extra:
+                    one(e, y, z, 1)
+                else:
+                    @pl.when(xh == 0)
                     def _():
-                        part_vec(slot, row, j).start()
-
-                    @pl.when(own_lane == j)
+                        one(e, y, z, 1)
+
+    def orbs(k, n):
+        piece = ro.at[k, pl.ds(0, bands * n)]
+        return remote(piece, piece, so.at[k], qo.at[k], (band, sib))
+
+    def send_vec(slot):
+        def one(i, x, k):
+            where, q = targets[i]
+            t = q + 8 * x + share_of * k
+            index = (i * 2 + xh) * bands + me
+
+            def go():
+                remote(vec.at[slot, tile_at(t)], rv.at[k, index], sv.at[k, slot], qv.at[k], (where + x, slot)).start()
+
+            if i > 0:
+                go()
+                return
+            home = jnp.logical_and(xh == x, slot == me)
+            pl.when(jnp.logical_not(home))(go)
+
+            @pl.when(home)
+            def _():
+                rv[k, index] = vec[slot, tile_at(t)]
+
+        for i in range(len(moves) - 1, -1, -1):
+            for x in range(2):
+                one(i, x, 0)
+                if x == 0:
+                    one(i, x, 1)
+                else:
+                    @pl.when(targets[i][1] + 8 < extra)
                     def _():
-                        r, l = cells(row, j)
-                        rv[band * bands + me] = vec[slot, r, l]
-
-        each(deep, one)
+                        one(i, x, 1)
+
+    def vecs(k, n, slot):
+        piece = rv.at[k, pl.ds(0, n)]
+        return remote(piece, piece, sv.at[k, slot], qv.at[k], (band, sib))
 
     def lay_orb():
         for r in range(pts):
@@ -195,62 +225,64 @@
                 for b in range(bands):
                     first = bands * (lanes * r + j) + b
                     rows_b = orb_ref[pl.ds(first, xs, stride=pts * lanes * bands), :]
-                    ox[b, xs * r : xs * r + xs, 128 * j : 128 * j + 128] = rows_b
-
-    def term(b, g):
-        return remote(gs.at[b * bands + g], gr.at[band * bands + me], sg, qg, (b, g))
+                    ox[0, b, pts * xs * j + xs * r : pts * xs * j + xs * r + xs, :] = rows_b
+
+    def lay_mate():
+        blk = 2 - xh
+        for j in range(lanes):
+            for r in range(pts):
+                st[j, rows * r : rows * r + rows, :] = buf[blk, me, r, :, 128 * j : 128 * j + 128]
+            for b in range(bands):
+                ox[1, b, pts * xs * j : pts * xs * (j + 1), :] = st[j, pl.ds(b, pts * xs, stride=bands), :]
+
+    def term(m, g):
+        return remote(gs.at[m * bands + g], gr.at[(m // 2 * 2 + xh) * bands + me], sg, qg, (sources[m // 2] + m % 2, g))
 
     def terms(n):
         return remote(gs.at[pl.ds(0, n)], gs.at[pl.ds(0, n)], sg, qg, (band, sib))
 
     def send_terms():
-        def one(k):
-            b = wrap(first_band + k, nband)
-
-            @pl.when(b != band)
-            def _():
-                for g in range(bands):
-                    term(b, g).start()
-
-            @pl.when(b == band)
-            def _():
-                for g in range(bands):
-                    @pl.when(me != g)
+        for m in range(share_of - 1, -1, -1):
+            for g in range(bands):
+                if m > 1:
+                    term(m, g).start()
+                else:
+                    home = jnp.logical_and(xh == m, me == g)
+
+                    @pl.when(jnp.logical_not(home))
                     def _():
-                        term(b, g).start()
-
-                    @pl.when(me == g)
+                        term(m, g).start()
+
+                    @pl.when(home)
                     def _():
-                        gr[band * bands + me] = gs[b * bands + g]
-
-        each(nband, one)
+                        gr[xh * bands + me] = gs[m * bands + g]
 
     def regroup(g):
-        sub = lax.broadcasted_iota(jnp.int32, (nall, nall), 0) % bands
+        sub = lax.broadcasted_iota(jnp.int32, g.shape, 0) % bands
         quarter = nall // bands
-        lane = lax.broadcasted_iota(jnp.int32, (nall, nall), 1) // quarter
+        lane = lax.broadcasted_iota(jnp.int32, g.shape, 1) // quarter
         out = g
         for d in range(1, bands):
-            moved = jnp.where(sub >= d, pltpu.roll(g, d, 0), pltpu.roll(g, nall + d - bands, 0))
+            moved = jnp.where(sub >= d, pltpu.roll(g, d, 0), pltpu.roll(g, g.shape[0] + d - bands, 0))
             moved = pltpu.roll(moved, nall - quarter * d, 1)
             out = jnp.where((sub + bands - lane) % bands == d, moved, out)
         return out
 
-    def take(src):
-        flat = src.reshape(nall * tile, 128)
-        return split(jnp.concatenate([flat[pl.ds(r, nall, stride=tile), :] for r in range(tile)], axis=1))
+    def take(src, n):
+        flat = src.reshape(n * tile, 128)
+        return split(jnp.concatenate([flat[pl.ds(r, n, stride=tile), :] for r in range(tile)], axis=1))
 
     def nt(a, b):
         return lax.dot_general(a, b, (((1,), (1,)), ((), ())), preferred_element_type=jnp.float32)
 
-    def tiles(n, sem):
-        return remote(rv.at[pl.ds(0, n)], rv.at[pl.ds(0, n)], sem, qv, (band, sib))
-
     barrier = pltpu.get_barrier_semaphore()
-    each(nband, lambda b: pl.semaphore_signal(barrier, inc=1, device_id=(b, cross), device_id_type=mesh_id))
-    for other in (sib, far):
-        pl.semaphore_signal(barrier, inc=1, device_id=(band, other), device_id_type=mesh_id)
-    pl.semaphore_wait(barrier, nband + 2)
+    def greet(device):
+        pl.semaphore_signal(barrier, inc=1, device_id=device, device_id_type=mesh_id)
+
+    for device in ((band, sib), (band, cross), (band, far), (above, cross), (below, cross)):
+        greet(device)
+    each(nband - 1, lambda k: greet((jnp.where(k >= band, k + 1, k), me)))
+    pl.semaphore_wait(barrier, nband + 4)
 
     for p in range(cuts):
         share(0, 1, me, p, cross).start()
@@ -404,35 +436,40 @@
         def _():
             for j in range(width // 128):
                 t = [acc[slot, j, pl.ds(b, pts * xs, stride=bands), :] for b in range(bands)]
-                vec[slot, :, 128 * j : 128 * j + 128] = -((t[0] + t[1]) + (t[2] + t[3]))
+                vec[slot, pts * xs * j : pts * xs * (j + 1), :] = -((t[0] + t[1]) + (t[2] + t[3]))
 
             send_vec(slot)
 
+    def product(k):
+        vh, vl = take(rv.at[k], share_of * bands)
+        return nt(vh, xo[k]) + nt(vh, xv[k]) + nt(vl, xo[k])
+
     def margin():
-        @pl.when(band < count)
-        def _():
-            remote(ro, ro, so, qo, (band, cross)).wait_recv()
-            xo[...], xv[...] = take(ro)
-            tiles(nall - 1, sv.at[0]).wait_recv()
-            vh, vl = take(rv)
-            g = nt(vh, xo[...]) + nt(vh, xv[...]) + nt(vl, xo[...])
-            g = regroup(g)
-            for n in range(nall):
-                gs[n] = g[n : n + 1]
-            send_terms()
-
+        others = 2 * (nband // 2 - 1)
+        orbs(0, others).wait_recv()
+        xo[0], xv[0] = take(ro.at[0], nall)
+
+        @pl.when(double)
+        def _():
+            orbs(1, others).wait_recv()
+            xo[1], xv[1] = take(ro.at[1], nall)
+
+        vecs(0, share_of * bands - 1, 0).wait_recv()
+        ga[...] = product(0)
+
+        @pl.when(double)
+        def _():
+            vecs(1, share_of * bands - 1, 0).wait_recv()
+            ga[...] += product(1)
+
+        g = regroup(ga[...])
+        for n in range(share_of * bands):
+            gs[n] = g[n : n + 1]
+        send_terms()
         collect()
         drain()
-
-        held = count * bands
-        @pl.when(band < count)
-        def _():
-            terms(held - 1).wait_recv()
-
-        @pl.when(band >= count)
-        def _():
-            terms(held).wait_recv()
-
+        held = share_of * bands
+        terms(held - 1).wait_recv()
         sums = [gr[n] for n in range(4)]
         for n in range(4, held):
             sums[n % 4] += gr[n]
@@ -447,13 +484,23 @@
             which = (chip + jnp.minimum(blk, 1) + h) % 2
             planar(0, ch, cl, keep_split, pl.ds(pl.multiple_of(which * 2 * rows, 32), 2 * rows))
 
-        each(2, half)
+        @pl.when(blk < 2)
+        def _():
+            each(2, half)
+
+        @pl.when(blk == 2)
+        def _():
+            each(4, lambda s: forward(blk, s))
+            planar(0, ch, cl, keep_split, slice(None))
+
+
+        xconv()
 
         @pl.when(blk == 1)
         def _():
             spread(2, 2, False)
-
-        xconv()
+            send_orb(ox.at[0], band)
+
         planar(1, zh, zl, keep, slice(None))
 
         @pl.when(blk == 0)
@@ -466,7 +513,8 @@
         def _():
             for p in range(cuts):
                 relay(2, me, p)
-            send_orb()
+            lay_mate()
+            send_orb(ox.at[1], band + 1 - 2 * xh)
 
         each(4, lambda s: inverse(blk, s))
 
@@ -475,7 +523,7 @@
     def place(slot, src):
         for r in range(pts):
             for j in range(width // 128):
-                piece = src[xs * r : xs * r + xs, 128 * j : 128 * j + 128]
+                piece = src[pts * xs * j + xs * r : pts * xs * j + xs * r + xs, :]
                 o_ref[pl.ds(bands * (width // 128 * r + j) + slot, xs, stride=pts * width // 128 * bands), :] = piece
 
     for slot in (cross, far, sib):
@@ -489,17 +537,39 @@
             place(k, recv[k])
 
     def drain():
-        remote(ox, ox, so, qo, (band, cross)).wait_send()
+        orbs(0, 2 * (nband // 2 - 1)).wait_send()
+        few = 4 * (extra - 8)
+
+        @pl.when(xh == 0)
+        def _():
+            orbs(1, 2 * (nband // 2 - 1)).wait_send()
+
+        @pl.when(jnp.logical_and(xh == 1, double))
+        def _():
+            orbs(1, few - 2).wait_send()
+
+        @pl.when(jnp.logical_and(xh == 1, jnp.logical_not(double)))
+        def _():
+            orbs(1, few).wait_send()
+
         for slot in range(4):
-            home = jnp.logical_and(band < count, (slot + 2) % 4 == me)
+            @pl.when(me == slot)
+            def _():
+                vecs(0, share_of - 1, slot).wait_send()
+
+            @pl.when(me != slot)
+            def _():
+                vecs(0, share_of, slot).wait_send()
+
+            home = jnp.logical_and(double, me == slot)
 
             @pl.when(home)
             def _():
-                tiles(count - 1, sv.at[slot]).wait_send()
+                vecs(1, extra - 1, slot).wait_send()
 
             @pl.when(jnp.logical_not(home))
             def _():
-                tiles(count, sv.at[slot]).wait_send()
+                vecs(1, extra, slot).wait_send()
 
         for p in range(cuts):
             for blk in range(3):
@@ -514,9 +584,7 @@
 
     margin()
 
-    @pl.when(band < count)
-    def _():
-        terms(nall - 1).wait_send()
+    terms(share_of * bands - 1).wait_send()
 
 
 def solve(orb, bands, groups, nband, ng):
@@ -532,10 +600,10 @@
     f32, bf16, dma = jnp.float32, jnp.bfloat16, pltpu.SemaphoreType.DMA
     tall = groups * rows
     xs = rows // bands
-    count, nall = orb.shape[0] // bands // 8, nband * bands
+    nall, flat = nband * bands, orb.shape[0] // bands
     vmem = pl.BlockSpec(memory_space=pltpu.VMEM)
     return pl.pallas_call(
-        functools.partial(solve_kernel, ng, count),
+        functools.partial(solve_kernel, ng),
         out_shape=[pltpu.VMEM(orb.shape, f32), pltpu.VMEM((bands, nall // groups), f32)],
         in_specs=[vmem] * 6,
         out_specs=[vmem] * 2,
@@ -547,13 +615,14 @@
             pltpu.VMEM((tall, total), f32),
             pltpu.VMEM((2, total, 2 * width), bf16), pltpu.VMEM((2, total, 2 * width), bf16),
             pltpu.VMEM((tall, total), f32),
-            pltpu.VMEM((groups, pts * xs, width), f32), pltpu.VMEM((groups, pts * xs, width), f32),
-            pltpu.VMEM((bands, pts * xs, width), f32),
-            pltpu.VMEM((nall, 8, 128), f32), pltpu.VMEM((nall, 8, 128), f32),
-            pltpu.VMEM((nall, 1024), bf16), pltpu.VMEM((nall, 1024), bf16),
-            pltpu.VMEM((nall, 1, nall), f32), pltpu.VMEM((count * groups, 1, nall), f32),
+            pltpu.VMEM((groups, flat, 128), f32), pltpu.VMEM((groups, flat, 128), f32),
+            pltpu.VMEM((2, bands, flat, 128), f32), pltpu.VMEM((width // 128, pts * rows, 128), f32),
+            pltpu.VMEM((2, nall, 8, 128), f32), pltpu.VMEM((2, nall // 2, 8, 128), f32),
+            pltpu.VMEM((2, nall, 1024), bf16), pltpu.VMEM((2, nall, 1024), bf16),
+            pltpu.VMEM((nall // 2, nall), f32),
+            pltpu.VMEM((nall // 2, 1, nall), f32), pltpu.VMEM((nall // 2, 1, nall), f32),
             dma((3, groups, 3)), dma((3, 3, 3)), dma((2, 3)), dma((2,)), dma((groups,)), dma((groups,)),
-            dma(()), dma((groups,)), dma(()), dma(()),
+            dma((2,)), dma((2, groups)), dma((2,)), dma((2,)),
             dma(()), dma(()),
         ],
         compiler_params=pltpu.CompilerParams(

time: 69.1 us -> 65.4 us (0.946)
  Pallas kernels: 67 us -> 63.3 us
    pallas_call x1, Pallas kernels: 67 us -> 63.3 us  [solve(): pl.pallas_call(functools.partial(solve_kernel, ng), out_shape=[pltpu.VMEM...]
where the time goes in v6:
time: 65.4 us; the launch traced here: 65.3 us
  Pallas kernels  63.3 us (97%)
  local copies, waits for them, and re-layouts  1.34 us (2%)
    pallas_call x1, Pallas kernels, solve(): pl.pallas_call(functools.partial(solve_kernel, ng), out_shape=[pltpu.VMEM...  63.3 us
    unnamed x2, local copies, waits for them, and re-layouts  1.34 us

profile of v6, /device:TPU:1, one launch (start us, length us, event | category | flops | bytes accessed | tf_op | source)
XLA Modules:
  0.0 65.3 jit_solution(2965549582797620545)
XLA Ops:
  0.6 63.3 %solve.1 = (f32[864,128]{1,0:T(8,128)S(1)}, f32[4,32]{1,0:T(4,128)S(1)}) custom-call(f32[864,128]{1,0:T(8,128)} %bitcast.13, f32[48,2304]{1,0:T(8,128)} %constant.10.clone.kt_ref, f32[48,768]{1,0:T(8,128)} %constant.11.clone.hz_ref, f32[2,48,768]{2,1,0:T(8,128)} %constant.12.clone.mix_ref, bf16[192,192]{1,0:T(8,128)(2,1)} %constant.13.clone.xh_ref, ...), custom_call_target="tpu_custom_call" | custom-call | flops 99999997952 | bytes 10000000 | tf_op jit(solution)/shard_map/solve/pallas_call | solution.py:605
  64.0 0.8 %copy.12 = f32[4,27648]{1,0:T(4,128)} copy(f32[4,27648]{1,0:T(4,128)S(1)} %bitcast.11) | data formatting | bytes 884736
  64.7 0.6 copy.13

commit v7 on v6

--- a/solution.py
+++ b/solution.py
@@ -77,10 +77,11 @@
     return jnp.dot(a, b, preferred_element_type=jnp.float32)
 
 
-def solve_kernel(ng, orb_ref, kt_ref, hz_ref, mix_ref, xh_ref, xl_ref, o_ref, m_ref,
+def solve_kernel(ng, orb_in, kt_in, hz_in, mix_in, xh_in, xl_in, o_ref, m_ref,
+                 orb_ref, kt_ref, hz_ref, mix_ref, xh_ref, xl_ref,
                  buf, amp, acc, ch, cl, zh, zl, cb, wh, wl, kx, vec, recv,
                  ox, st, ro, rv, xo, xv, ga, gs, gr,
-                 rsem, ssem, nsem, fsem, osem, orsem, so, sv, qo, qv, sg, qg):
+                 rsem, ssem, nsem, fsem, osem, orsem, so, sv, qo, qv, sg, qg, ls):
     pts, rows, width = buf.shape[2:]
     bands, step = 4, ng // PTS
     xs = rows // bands
@@ -124,17 +125,6 @@
 
         lax.fori_loop(0, n, one, 0)
 
-    def lay_own(q):
-        for h in range(2):
-            for r in range(pts):
-                for j in range(width // 128):
-                    unit = ((2 * q + h) * pts + r) * (width // 128) + j
-                    piece = orb_ref[bands * unit : bands * unit + bands, :]
-                    at = (me, r, pl.ds(8 * q + 4 * h, bands), pl.ds(128 * j, 128))
-                    buf[(0,) + at] = piece
-
-    for q in range(xs // 2):
-        lay_own(q)
 
     lanes = width // 128
     tile, nall = 8, nband * bands
@@ -282,6 +272,23 @@
     for device in ((band, sib), (band, cross), (band, far), (above, cross), (below, cross)):
         greet(device)
     each(nband - 1, lambda k: greet((jnp.where(k >= band, k + 1, k), me)))
+    pairs = ((orb_in, orb_ref), (hz_in, hz_ref), (mix_in, mix_ref), (kt_in, kt_ref), (xh_in, xh_ref), (xl_in, xl_ref))
+    loads = [pltpu.make_async_copy(src, dst, ls.at[n]) for n, (src, dst) in enumerate(pairs)]
+    for load in loads:
+        load.start()
+    loads[0].wait()
+
+    def lay_own(q):
+        for h in range(2):
+            for r in range(pts):
+                for j in range(width // 128):
+                    unit = ((2 * q + h) * pts + r) * (width // 128) + j
+                    piece = orb_ref[bands * unit : bands * unit + bands, :]
+                    at = (me, r, pl.ds(8 * q + 4 * h, bands), pl.ds(128 * j, 128))
+                    buf[(0,) + at] = piece
+
+    for q in range(xs // 2):
+        lay_own(q)
     pl.semaphore_wait(barrier, nband + 4)
 
     for p in range(cuts):
@@ -302,6 +309,8 @@
 
         lax.fori_loop(first, last, one, 0)
 
+    for load in loads[1:]:
+        load.wait()
     weights(0, 2 * step, width)
     weights(2 * step, PTS * step, 2 * width)
 
@@ -356,16 +365,13 @@
             for p in range(cuts):
                 relay(0, cross, p)
                 if p == 0:
+                    near(2, 0).start()
                     onward(1, 0).start()
-                    for k in range(cuts):
+                    for k in range(1, cuts):
                         near(2, k).start()
                 if p == cuts - 1:
                     onward(2, p).start()
                 spread(1, p, p > 0)
-
-        @pl.when(jnp.logical_and(blk == 1, s == 2))
-        def _():
-            spread(2, 1, True)
 
         @pl.when(s % 2 == 1)
         def _():
@@ -494,7 +500,15 @@
             planar(0, ch, cl, keep_split, slice(None))
 
 
+        @pl.when(blk == 1)
+        def _():
+            spread(2, 1, True)
+
         xconv()
+
+        @pl.when(blk == 0)
+        def _():
+            spread(2, 0, True)
 
         @pl.when(blk == 1)
         def _():
@@ -505,7 +519,6 @@
 
         @pl.when(blk == 0)
         def _():
-            spread(2, 0, True)
             for p in range(cuts):
                 relay(1, me, p)
 
@@ -605,9 +618,10 @@
     return pl.pallas_call(
         functools.partial(solve_kernel, ng),
         out_shape=[pltpu.VMEM(orb.shape, f32), pltpu.VMEM((bands, nall // groups), f32)],
-        in_specs=[vmem] * 6,
+        in_specs=[pl.BlockSpec(memory_space=pltpu.HBM)] * 6,
         out_specs=[vmem] * 2,
         scratch_shapes=[
+            pltpu.VMEM(orb.shape, f32), *[pltpu.VMEM(c.shape, c.dtype) for c in consts],
             pltpu.VMEM((3,) + full, f32), pltpu.VMEM(full, f32),
             pltpu.VMEM((groups, width // 128, pts * rows, 128), f32),
             pltpu.VMEM((tall, total), bf16), pltpu.VMEM((tall, total), bf16),
@@ -623,7 +637,7 @@
             pltpu.VMEM((nall // 2, 1, nall), f32), pltpu.VMEM((nall // 2, 1, nall), f32),
             dma((3, groups, 3)), dma((3, 3, 3)), dma((2, 3)), dma((2,)), dma((groups,)), dma((groups,)),
             dma((2,)), dma((2, groups)), dma((2,)), dma((2,)),
-            dma(()), dma(()),
+            dma(()), dma(()), dma((6,)),
         ],
         compiler_params=pltpu.CompilerParams(
             vmem_limit_bytes=56 * 1024 * 1024, collective_id=0, has_side_effects=True

time: 65.4 us -> 63.8 us (0.976)
  Pallas kernels: 63.3 us -> 61.7 us
    pallas_call x1, Pallas kernels: 63.3 us -> 61.7 us  [solve(): pl.pallas_call(functools.partial(solve_kernel, ng), out_shape=[pltpu.VMEM...]
where the time goes in v7:
time: 63.8 us; the launch traced here: 63.7 us
  Pallas kernels  61.7 us (97%)
  local copies, waits for them, and re-layouts  1.34 us (2%)
  between operations  0.64 us (1%)
    pallas_call x1, Pallas kernels, solve(): pl.pallas_call(functools.partial(solve_kernel, ng), out_shape=[pltpu.VMEM...  61.7 us
    unnamed x2, local copies, waits for them, and re-layouts  1.34 us

profile of v7, /device:TPU:1, one launch (start us, length us, event | category | flops | bytes accessed | tf_op | source)
XLA Modules:
  0.0 63.7 jit_solution(7216228007831024552)
XLA Ops:
  0.6 61.7 %solve.1 = (f32[864,128]{1,0:T(8,128)S(1)}, f32[4,32]{1,0:T(4,128)S(1)}) custom-call(f32[864,128]{1,0:T(8,128)} %bitcast.13, f32[48,2304]{1,0:T(8,128)} %constant.10.clone.kt_in, f32[48,768]{1,0:T(8,128)} %constant.11.clone.hz_in, f32[2,48,768]{2,1,0:T(8,128)} %constant.12.clone.mix_in, bf16[192,192]{1,0:T(8,128)(2,1)} %constant.13.clone.xh_in, ...), custom_call_target="tpu_custom_call" | custom-call | flops 99999997952 | bytes 10000000 | tf_op jit(solution)/shard_map/solve/pallas_call | solution.py:618
  62.3 0.8 %copy.12 = f32[4,27648]{1,0:T(4,128)} copy(f32[4,27648]{1,0:T(4,128)S(1)} %bitcast.11) | data formatting | bytes 884736
  63.1 0.6 copy.13

commit v8 on v7

--- a/solution.py
+++ b/solution.py
@@ -472,10 +472,10 @@
         for n in range(share_of * bands):
             gs[n] = g[n : n + 1]
         send_terms()
-        collect()
         drain()
         held = share_of * bands
         terms(held - 1).wait_recv()
+        collect()
         sums = [gr[n] for n in range(4)]
         for n in range(4, held):
             sums[n % 4] += gr[n]

time: 63.8 us -> 63.8 us (level)
  no operation moved by 1% of the time
where the time goes in v8:
time: 63.8 us; the launch traced here: 63.7 us
  Pallas kernels  61.7 us (97%)
  local copies, waits for them, and re-layouts  1.34 us (2%)
  between operations  0.64 us (1%)
    pallas_call x1, Pallas kernels, solve(): pl.pallas_call(functools.partial(solve_kernel, ng), out_shape=[pltpu.VMEM...  61.7 us
    unnamed x2, local copies, waits for them, and re-layouts  1.34 us

profile of v8, /device:TPU:1, one launch (start us, length us, event | category | flops | bytes accessed | tf_op | source)
XLA Modules:
  0.0 63.7 jit_solution(4108361695979562426)
XLA Ops:
  0.6 61.7 %solve.1 = (f32[864,128]{1,0:T(8,128)S(1)}, f32[4,32]{1,0:T(4,128)S(1)}) custom-call(f32[864,128]{1,0:T(8,128)} %bitcast.13, f32[48,2304]{1,0:T(8,128)} %constant.10.clone.kt_in, f32[48,768]{1,0:T(8,128)} %constant.11.clone.hz_in, f32[2,48,768]{2,1,0:T(8,128)} %constant.12.clone.mix_in, bf16[192,192]{1,0:T(8,128)(2,1)} %constant.13.clone.xh_in, ...), custom_call_target="tpu_custom_call" | custom-call | flops 99999997952 | bytes 10000000 | tf_op jit(solution)/shard_map/solve/pallas_call | solution.py:618
  62.4 0.8 %copy.12 = f32[4,27648]{1,0:T(4,128)} copy(f32[4,27648]{1,0:T(4,128)S(1)} %bitcast.11) | data formatting | bytes 884736
  63.1 0.6 copy.13
